TPU v7x, 256 devices: a whole 4x4x8 slice. The times are simulated.
256 devices in a mesh: dp: 8 (over z), ctx: 32 (over y, x, core).
Axes of the slice: x: 4, y: 4, z: 8, core: 2. Of those that a mesh axis runs over, the one named last changes fastest.
Arguments:
- queries: bfloat16 [65536, 2048], P(('dp', 'ctx')), parts along dimension 0, may hold values from -256 to 256
- key_rows: bfloat16 [65536, 2048], P(('dp', 'ctx')), parts along dimension 0, may hold values from -256 to 256
- values: bfloat16 [65536, 2048], P(('dp', 'ctx')), parts along dimension 0, may hold values from -6 to 6
- inner_rows: bfloat16 [65536, 4096], P(('dp', 'ctx')), parts along dimension 0, may hold values from -6 to 6
- conv_weight: float32 [4, 4096], replicated, may hold values from -3 to 3
- conv_bias: float32 [4096], replicated, may hold values from -3 to 3
- segment_ids: int32 [65536], P(('dp', 'ctx')), parts along dimension 0, may hold values from 0 to 3, never falling along the last dimension, each value on 1 to 4096 neighbouring positions
- block_reach: int32 [512], P(('dp', 'ctx')), parts along dimension 0, may hold values from 128 to 2048
- owner_counts: int32 [256], P('dp'), parts along dimension 0, may hold values from 1 to 3, as said below
Outputs:
- attn_owned: bfloat16 [98304, 2048], P(('dp', 'ctx')), parts along dimension 0
- conv_owned: bfloat16 [98304, 4096], P(('dp', 'ctx')), parts along dimension 0
There are 8 independent parts, one for each index of `dp`. A program takes and returns all parts, laid end to end along the dimension named above; an argument that names none is the same for every part. Nothing has to cross between parts.
Inputs may be any that keep to these rules, and one draw needn't show every extreme that they name: `owner_counts`: the counts sum to 64. The blocks owned by the devices before device d number at least d * 2 and at most d * 2 + 1.
All inputs are finite; a program needn't handle non-finite values.
Results may differ from a plain program's by a relative error of at most 0.0047.
Values may be sent and summed in bfloat16 or wider, within the bound.
No kernel may reach another device: no remote copies, remote signals or barrier semaphores. Data moves between devices by JAX's collectives and lax.ppermute only.
A program may use at most 192 MiB of HBM per device.

v0:
```python
import math

import jax
import jax.numpy as jnp
from jax import lax
from jax.sharding import PartitionSpec as P

HEADS = 16
D_HEAD = 128
WINDOW = 2048
BLOCK = 128
KERNEL = 4


masked_score = -1e30


def from_behind(block, axis, distance):
    devices = range(lax.axis_size(axis))
    route = [(i - distance, i) for i in devices if i - distance in devices]
    return lax.ppermute(block, axis, route)


def attend(query_rows, key_span, value_span, query_seg, key_seg, block_first, reach_value):
    query_pos = block_first + jnp.arange(BLOCK, dtype=jnp.int32)
    key_pos = block_first - WINDOW + jnp.arange(WINDOW + BLOCK, dtype=jnp.int32)
    allowed = (key_pos[None, :] <= query_pos[:, None]) & (
        key_pos[None, :] > query_pos[:, None] - WINDOW
    )
    allowed = allowed & (key_pos[None, :] >= block_first - reach_value) & (key_pos[None, :] >= 0)
    allowed = allowed & (key_seg[None, :] == query_seg[:, None])
    heads_q = query_rows.reshape(BLOCK, HEADS, D_HEAD)
    heads_k = key_span.reshape(WINDOW + BLOCK, HEADS, D_HEAD)
    heads_v = value_span.reshape(WINDOW + BLOCK, HEADS, D_HEAD)
    scores = jnp.einsum("qhd,khd->hqk", heads_q, heads_k, preferred_element_type=jnp.float32) * (
        1.0 / math.sqrt(D_HEAD)
    )
    scores = jnp.where(allowed[None], scores, masked_score)
    row_top = jnp.max(scores, axis=2, keepdims=True)
    lifted = jnp.where(allowed[None], jnp.exp(scores - row_top), 0.0)
    weights = (lifted / jnp.sum(lifted, axis=2, keepdims=True)).astype(jnp.bfloat16)
    mixed = jnp.einsum("hqk,khd->qhd", weights, heads_v, preferred_element_type=jnp.float32)
    return mixed.reshape(BLOCK, HEADS * D_HEAD).astype(jnp.bfloat16)


def convolve(ext_rows, ext_seg, ext_pos, conv_weight, conv_bias, row_count):
    lag = KERNEL - 1
    running = jnp.zeros((row_count, conv_bias.shape[0]), jnp.float32) + conv_bias[None, :]
    for offset in range(KERNEL):
        shifted = ext_rows[lag - offset : lag - offset + row_count].astype(jnp.float32)
        usable = (ext_seg[lag - offset : lag - offset + row_count] == ext_seg[lag:]) & (
            ext_pos[lag - offset : lag - offset + row_count] >= 0
        )
        running = running + conv_weight[offset][None, :] * jnp.where(usable[:, None], shifted, 0.0)
    return jax.nn.silu(running).astype(jnp.bfloat16)


def pad_back(array, total):
    return jnp.pad(array, ((0, total - array.shape[0]),) + ((0, 0),) * (array.ndim - 1))


def shards(
    queries,
    key_rows,
    values,
    inner_rows,
    conv_weight,
    conv_bias,
    segment_ids,
    block_reach,
    owner_counts,
):
    here_index = lax.axis_index("ctx")
    row_count = queries.shape[0]
    features = queries.shape[1]
    channels = inner_rows.shape[1]
    per_device = row_count // BLOCK
    most_blocks = per_device + per_device // 2
    back = WINDOW // row_count
    lag = KERNEL - 1
    cut = row_count // 2
    keep = row_count - cut
    starts = jnp.cumsum(owner_counts) - owner_counts
    first_block = starts[here_index]
    own_blocks = owner_counts[here_index]
    live = jnp.arange(most_blocks * BLOCK, dtype=jnp.int32) < own_blocks * BLOCK
    far_keys = []
    far_values = []
    far_segments = []
    for distance in range(back, 0, -1):
        received = from_behind((key_rows, values, segment_ids), "ctx", distance)
        far_keys.append(received[0])
        far_values.append(received[1])
        far_segments.append(received[2])
    key_buffer = jnp.concatenate(far_keys + [key_rows], axis=0)
    value_buffer = jnp.concatenate(far_values + [values], axis=0)
    segment_buffer = jnp.concatenate(far_segments + [segment_ids], axis=0)
    key_anchor = (here_index - back) * row_count
    tail_rows, tail_segments = from_behind(
        (inner_rows[row_count - lag :], segment_ids[row_count - lag :]), "ctx", 1
    )

    def own_block(slot_index):
        local_first = slot_index * BLOCK
        block_first = here_index * row_count + local_first
        key_at = block_first - WINDOW - key_anchor
        return attend(
            lax.dynamic_slice_in_dim(queries, local_first, BLOCK, 0),
            lax.dynamic_slice_in_dim(key_buffer, key_at, WINDOW + BLOCK, 0),
            lax.dynamic_slice_in_dim(value_buffer, key_at, WINDOW + BLOCK, 0),
            lax.dynamic_slice_in_dim(segment_ids, local_first, BLOCK, 0),
            lax.dynamic_slice_in_dim(segment_buffer, key_at, WINDOW + BLOCK, 0),
            block_first,
            block_reach[slot_index],
        )

    attention_local = lax.map(own_block, jnp.arange(per_device, dtype=jnp.int32)).reshape(
        row_count, features
    )
    conv_local = convolve(
        jnp.concatenate([tail_rows, inner_rows], axis=0),
        jnp.concatenate([tail_segments, segment_ids], axis=0),
        here_index * row_count - lag + jnp.arange(row_count + lag, dtype=jnp.int32),
        conv_weight,
        conv_bias,
        row_count,
    )
    above = from_behind((attention_local[:keep], conv_local[:keep]), "ctx", -1)
    attention_near = jnp.concatenate(
        [
            attention_local,
            pad_back(above[0], row_count),
            jnp.zeros((row_count, features), jnp.bfloat16),
        ],
        axis=0,
    )
    conv_near = jnp.concatenate(
        [conv_local, pad_back(above[1], row_count), jnp.zeros((row_count, channels), jnp.bfloat16)],
        axis=0,
    )
    offset_rows = first_block * BLOCK - here_index * row_count
    attention_owned = lax.dynamic_slice_in_dim(attention_near, offset_rows, most_blocks * BLOCK, 0)
    conv_owned_rows = lax.dynamic_slice_in_dim(conv_near, offset_rows, most_blocks * BLOCK, 0)
    attention_owned = jnp.where(live[:, None], attention_owned, 0)
    conv_owned_rows = jnp.where(live[:, None], conv_owned_rows, 0)
    return (attention_owned, conv_owned_rows)


def solution(mesh):
    return jax.shard_map(
        shards,
        mesh=mesh,
        in_specs=(
            P(("dp", "ctx"), None),
            P(("dp", "ctx"), None),
            P(("dp", "ctx"), None),
            P(("dp", "ctx"), None),
            P(),
            P(),
            P(("dp", "ctx")),
            P(("dp", "ctx")),
            P("dp"),
        ),
        out_specs=(P(("dp", "ctx"), None), P(("dp", "ctx"), None)),
        check_vma=False,
    )
```

profile of v0, /device:TPU:104, one launch (start us, length us, event | category | flops | bytes accessed | tf_op | source)
XLA Modules:
  0.0 509.3 jit_solution(5196088463897529394)
XLA Ops:
  0.6 1.5 copy.34
  2.1 3.5 collective-permute-start.16
  5.6 3.8 collective-permute-start.17
  9.4 3.5 collective-permute-start.18
  12.9 2.5 collective-permute-start.19
  16.2 2.3 collective-permute-start.25
  18.5 1.5 copy.25
  21.5 1.3 dynamic_slice.62
  25.3 1.1 fusion.30
  26.3 0.9 slice.65
  27.9 1.9 collective-permute-start.8
  31.3 55.0 %collective-permute-done.8 = s32[256]{0:T(256)S(1)} collective-permute-done((s32[256]{0:T(256)}, s32[256]{0:T(256)S(1)}, u32[]{:S(2)}, u32[]{:S(2)}) %collective-permute-start.8) | collective-permute-done | bytes 1056 | tf_op jit(solution)/shard_map/ppermute | solution.py:21
  86.3 1.9 collective-permute-start.9
  88.3 10.1 %collective-permute-done.9 = s32[256]{0:T(256)S(1)} collective-permute-done((s32[256]{0:T(256)}, s32[256]{0:T(256)S(1)}, u32[]{:S(2)}, u32[]{:S(2)}) %collective-permute-start.9) | collective-permute-done | bytes 1056 | tf_op jit(solution)/shard_map/ppermute | solution.py:21
  98.4 1.9 collective-permute-start.10
  100.3 5.2 %collective-permute-done.10 = s32[256]{0:T(256)S(1)} collective-permute-done((s32[256]{0:T(256)}, s32[256]{0:T(256)S(1)}, u32[]{:S(2)}, u32[]{:S(2)}) %collective-permute-start.10) | collective-permute-done | bytes 1056 | tf_op jit(solution)/shard_map/ppermute | solution.py:21
  105.5 5.7 %collective-permute-start.11 = (s32[256]{0:T(256)}, s32[256]{0:T(256)S(1)}, u32[]{:S(2)}, u32[]{:S(2)}) collective-permute-start(s32[256]{0:T(256)} %param.17), channel_id=1, source_target_pairs={{0,5},{1,6},{2,7},{3,8},{4,9},{5,10},{6,11},{7,12},{8,13},{9,14},{... | collective-permute-start | bytes 3080 | tf_op jit(solution)/shard_map/ppermute | solution.py:21
  111.2 1.5 collective-permute-done.11
  112.7 5.9 %collective-permute-start.12 = (s32[256]{0:T(256)}, s32[256]{0:T(256)S(1)}, u32[]{:S(2)}, u32[]{:S(2)}) collective-permute-start(s32[256]{0:T(256)} %param.17), channel_id=1, source_target_pairs={{0,4},{1,5},{2,6},{3,7},{4,8},{5,9},{6,10},{7,11},{8,12},{9,13},{1... | collective-permute-start | bytes 3080 | tf_op jit(solution)/shard_map/ppermute | solution.py:21
  118.6 2.1 collective-permute-done.12
  120.7 4.7 collective-permute-start.13
  125.4 2.8 collective-permute-done.13
  128.2 4.4 collective-permute-start.14
  132.7 3.4 collective-permute-done.14
  136.0 2.1 collective-permute-start.15
  138.1 5.1 collective-permute-done.15
  143.2 1.9 collective-permute-start.26
  145.8 4.7 collective-permute-done.26
  150.5 1.9 collective-permute-start.20
  152.5 8.8 %multiply_convert_fusion = bf16[256,4096]{1,0:T(8,128)(2,1)S(1)} fusion(bf16[256,4096]{1,0:T(8,128)(2,1)} %param.14, bf16[3,4096]{1,0:T(4,128)(2,1)S(1)} %collective-permute-done.26, f32[4096]{0:T(1024)S(1)} %bitcast.48, f32[4096]{0:T(1024)S(1)} %bitcast.49, f32[4096]{0:T(1024)S(1)} %bitcast.47, f32[4096]{0:T(1024)S(1)} %bitcast.46, f32[4096]{0:T(1024)} %param.16, ...), kind=kLoop, calls=%fused_computation.30 | loop fusion | flops 31457280 | bytes 4301824 | tf_op jit(solution)/shard_map/convert_element_type | solution.py:55
  161.2 1.2 slice.80
  162.5 1.9 collective-permute-start.21
  164.4 1.3 constant_dynamic-update-slice_fusion.19
  165.7 1.9 collective-permute-start.22
  167.6 1.3 constant_dynamic-update-slice_fusion.18
  168.9 6.4 %collective-permute-start.23 = (bf16[256,2048]{0,1:T(8,128)(2,1)S(1)}, bf16[256,2048]{0,1:T(8,128)(2,1)S(1)}, u32[]{:S(2)}, u32[]{:S(2)}) collective-permute-start(bf16[256,2048]{0,1:T(8,128)(2,1)S(1)} %copy.34), channel_id=1, source_target_pairs={{0,1},{1,2},{2,3},{3,4},{4,5},{5,6},{6,7},{7,8},{8,9},{9,10},{10,1... | collective-permute-start | bytes 3145736 | tf_op jit(solution)/shard_map/ppermute | solution.py:21
  175.4 1.3 constant_dynamic-update-slice_fusion.17
  176.7 3.5 collective-permute-start
  181.0 3.2 collective-permute-start.1
  184.3 11.2 %collective-permute-done.21 = bf16[256,2048]{0,1:T(8,128)(2,1)S(1)} collective-permute-done((bf16[256,2048]{0,1:T(8,128)(2,1)S(1)}, bf16[256,2048]{0,1:T(8,128)(2,1)S(1)}, u32[]{:S(2)}, u32[]{:S(2)}) %collective-permute-start.21) | collective-permute-done | bytes 1048608 | tf_op jit(solution)/shard_map/ppermute | solution.py:21
  195.4 30.3 %collective-permute-start.2 = (bf16[256,2048]{0,1:T(8,128)(2,1)S(1)}, bf16[256,2048]{0,1:T(8,128)(2,1)S(1)}, u32[]{:S(2)}, u32[]{:S(2)}) collective-permute-start(bf16[256,2048]{0,1:T(8,128)(2,1)S(1)} %copy.25), channel_id=1, source_target_pairs={{0,6},{1,7},{2,8},{3,9},{4,10},{5,11},{6,12},{7,13},{8,14},{9,15},... | collective-permute-start | bytes 3145736 | tf_op jit(solution)/shard_map/ppermute | solution.py:21
  225.9 50.9 %collective-permute-done.22 = bf16[256,2048]{0,1:T(8,128)(2,1)S(1)} collective-permute-done((bf16[256,2048]{0,1:T(8,128)(2,1)S(1)}, bf16[256,2048]{0,1:T(8,128)(2,1)S(1)}, u32[]{:S(2)}, u32[]{:S(2)}) %collective-permute-start.22) | collective-permute-done | bytes 1048608 | tf_op jit(solution)/shard_map/ppermute | solution.py:21
  276.8 1.9 collective-permute-start.3
  278.8 1.9 collective-permute-start.4
  280.9 52.2 %collective-permute-done = bf16[256,2048]{0,1:T(8,128)(2,1)S(1)} collective-permute-done((bf16[256,2048]{0,1:T(8,128)(2,1)S(1)}, bf16[256,2048]{0,1:T(8,128)(2,1)S(1)}, u32[]{:S(2)}, u32[]{:S(2)}) %collective-permute-start) | collective-permute-done | bytes 1048608 | tf_op jit(solution)/shard_map/ppermute | solution.py:21
  333.1 1.9 collective-permute-start.5
  335.0 31.6 %collective-permute-done.1 = bf16[256,2048]{0,1:T(8,128)(2,1)S(1)} collective-permute-done((bf16[256,2048]{0,1:T(8,128)(2,1)S(1)}, bf16[256,2048]{0,1:T(8,128)(2,1)S(1)}, u32[]{:S(2)}, u32[]{:S(2)}) %collective-permute-start.1) | collective-permute-done | bytes 1048608 | tf_op jit(solution)/shard_map/ppermute | solution.py:21
  366.7 1.9 collective-permute-start.6
  368.7 1.9 collective-permute-start.7
  370.7 5.9 %collective-permute-start.27 = (bf16[128,4096]{1,0:T(8,128)(2,1)}, bf16[128,4096]{1,0:T(8,128)(2,1)}, u32[]{:S(2)}, u32[]{:S(2)}) collective-permute-start(bf16[128,4096]{1,0:T(8,128)(2,1)} %slice.80), channel_id=1, source_target_pairs={{1,0},{2,1},{3,2},{4,3},{5,4},{6,5},{7,6},{8,7},{9,8},{10,9},{11,1... | collective-permute-start | bytes 3145736 | tf_op jit(solution)/shard_map/ppermute | solution.py:21
  376.9 19.8 %collective-permute-done.6 = bf16[256,2048]{0,1:T(8,128)(2,1)S(1)} collective-permute-done((bf16[256,2048]{0,1:T(8,128)(2,1)S(1)}, bf16[256,2048]{0,1:T(8,128)(2,1)S(1)}, u32[]{:S(2)}, u32[]{:S(2)}) %collective-permute-start.6) | collective-permute-done | bytes 1048608 | tf_op jit(solution)/shard_map/ppermute | solution.py:21
  396.8 9.3 %collective-permute-done.7 = bf16[256,2048]{0,1:T(8,128)(2,1)S(1)} collective-permute-done((bf16[256,2048]{0,1:T(8,128)(2,1)S(1)}, bf16[256,2048]{0,1:T(8,128)(2,1)S(1)}, u32[]{:S(2)}, u32[]{:S(2)}) %collective-permute-start.7) | collective-permute-done | bytes 1048608 | tf_op jit(solution)/shard_map/ppermute | solution.py:21
  406.2 3.6 copy-done.1
  409.8 87.5 %while.13 = (s32[]{:T(128)}, bf16[2,128,2048]{2,1,0:T(8,128)(2,1)}, s32[2]{0:T(128)S(1)}, s32[]{:T(128)}, s32[]{:T(128)}, /*index=5*/bf16[2304,2048]{0,1:T(8,128...) while((s32[]{:T(128)}, bf16[2,128,2048]{2,1,0:T(8,128)(2,1)}, ...), condition=%wide.region_3.4_spmd, body=%wide.region_0.3_spmd.sunk | while | flops 2315119616 | bytes 99196312 | solution.py:117
  415.1 12.0 %constant_dynamic-slice_fusion.5 = (bf16[2176,2048]{0,1:T(8,128)(2,1)}, bf16[2176,2048]{0,1:T(8,128)(2,1)}) fusion(bf16[2304,2048]{0,1:T(8,128)(2,1)} %get-tuple-element.350, s32[]{:T(128)S(6)} %select_n.98, bf16[2304,2048]{0,1:T(8,128)(2,1)} %get-tuple-element.345), kind=kLoop, calls=%fused_computation.16.clone.1 | loop fusion | bytes 35651588 | tf_op jit(solution)/shard_map/while/body/eval_jaxpr/dynamic_slice | solution.py:109
  427.5 13.6 %fusion.46 = (f32[16,128]{1,0:T(8,128)S(1)}, f32[16,128,2176]{2,1,0:T(8,128)}) fusion(pred[128,2176]{1,0:T(8,128)(4,1)S(1)} %compare_and_fusion.5, bf16[128,16,128]{0,2,1:T(8,128)(2,1)S(1)} %bitcast.43, bf16[2176,16,128]{0,2,1:T(8,128)(2,1)} %bitcast.42), kind=kOutput, calls=%fused_computation.85.clone.1 | convolution fusion | flops 1163135104 | bytes 27549696 | tf_op jit(solution)/shard_map/while/body/eval_jaxpr/sub | solution.py:40
  441.1 11.4 %fusion.47 = bf16[16,128,128]{2,1,0:T(8,128)(2,1)S(1)} fusion(bf16[2176,16,128]{0,2,1:T(8,128)(2,1)} %bitcast.41, f32[16,128,2176]{2,1,0:T(8,128)} %get-tuple-element.302, f32[16,128]{1,0:T(8,128)S(1)} %get-tuple-element.303), kind=kOutput, calls=%fused_computation.10.clone.1 | convolution fusion | flops 1150025728 | bytes 27271168 | tf_op jit(solution)/shard_map/while/body/eval_jaxpr/hqk,khd->qhd/dot_general | solution.py:42
  458.8 12.0 %constant_dynamic-slice_fusion.5 = (bf16[2176,2048]{0,1:T(8,128)(2,1)}, bf16[2176,2048]{0,1:T(8,128)(2,1)}) fusion(bf16[2304,2048]{0,1:T(8,128)(2,1)} %get-tuple-element.350, s32[]{:T(128)S(6)} %select_n.98, bf16[2304,2048]{0,1:T(8,128)(2,1)} %get-tuple-element.345), kind=kLoop, calls=%fused_computation.16.clone.1 | loop fusion | bytes 35651588 | tf_op jit(solution)/shard_map/while/body/eval_jaxpr/dynamic_slice | solution.py:109
  471.2 13.6 %fusion.46 = (f32[16,128]{1,0:T(8,128)S(1)}, f32[16,128,2176]{2,1,0:T(8,128)}) fusion(pred[128,2176]{1,0:T(8,128)(4,1)S(1)} %compare_and_fusion.5, bf16[128,16,128]{0,2,1:T(8,128)(2,1)S(1)} %bitcast.43, bf16[2176,16,128]{0,2,1:T(8,128)(2,1)} %bitcast.42), kind=kOutput, calls=%fused_computation.85.clone.1 | convolution fusion | flops 1163135104 | bytes 27549696 | tf_op jit(solution)/shard_map/while/body/eval_jaxpr/sub | solution.py:40
  484.8 11.4 %fusion.47 = bf16[16,128,128]{2,1,0:T(8,128)(2,1)S(1)} fusion(bf16[2176,16,128]{0,2,1:T(8,128)(2,1)} %bitcast.41, f32[16,128,2176]{2,1,0:T(8,128)} %get-tuple-element.302, f32[16,128]{1,0:T(8,128)S(1)} %get-tuple-element.303), kind=kOutput, calls=%fused_computation.10.clone.1 | convolution fusion | flops 1150025728 | bytes 27271168 | tf_op jit(solution)/shard_map/while/body/eval_jaxpr/hqk,khd->qhd/dot_general | solution.py:42
  497.3 1.2 slice_bitcast_fusion
  498.4 1.9 collective-permute-start.24
  500.4 6.8 %fusion.19 = bf16[384,4096]{1,0:T(8,128)(2,1)} fusion(s32[]{:T(128)S(6)} %select_n.69, bf16[256,4096]{1,0:T(8,128)(2,1)S(1)} %copy-done.3, bf16[128,4096]{1,0:T(8,128)(2,1)} %collective-permute-done.27, pred[384]{0:T(512)(128)(4,1)S(1)} %copy-done.8, bf16[384]{0:T(512)(128)(2,1)S(1)} %copy-done.6), kind=kLoop, calls=%fused_computation.33 | loop fusion | flops 18874368 | bytes 6293632 | tf_op jit(solution)/shard_map/jit(_where)/select_n | solution.py:145
  507.2 2.1 fusion.28
  (97 shorter events, 15.0 us)
Async XLA Ops:
  2.1 160.4 %collective-permute-start.16 = (bf16[256,2048]{0,1:T(8,128)(2,1)S(1)}, bf16[256,2048]{0,1:T(8,128)(2,1)}, u32[]{:S(2)}, u32[]{:S(2)}) collective-permute-start(bf16[256,2048]{0,1:T(8,128)(2,1)S(1)} %copy.34), channel_id=1, source_target_pairs={{0,8},{1,9},{2,10},{3,11},{4,12},{5,13},{6,14},{7,15},{8,16},{9,17... | collective-permute-start | bytes 3145736 | tf_op jit(solution)/shard_map/ppermute | solution.py:21
  5.6 160.1 %collective-permute-start.17 = (bf16[256,2048]{0,1:T(8,128)(2,1)S(1)}, bf16[256,2048]{0,1:T(8,128)(2,1)}, u32[]{:S(2)}, u32[]{:S(2)}) collective-permute-start(bf16[256,2048]{0,1:T(8,128)(2,1)S(1)} %copy.34), channel_id=1, source_target_pairs={{0,7},{1,8},{2,9},{3,10},{4,11},{5,12},{6,13},{7,14},{8,15},{9,16}... | collective-permute-start | bytes 3145736 | tf_op jit(solution)/shard_map/ppermute | solution.py:21
  9.4 159.5 %collective-permute-start.18 = (bf16[256,2048]{0,1:T(8,128)(2,1)S(1)}, bf16[256,2048]{0,1:T(8,128)(2,1)}, u32[]{:S(2)}, u32[]{:S(2)}) collective-permute-start(bf16[256,2048]{0,1:T(8,128)(2,1)S(1)} %copy.34), channel_id=1, source_target_pairs={{0,6},{1,7},{2,8},{3,9},{4,10},{5,11},{6,12},{7,13},{8,14},{9,15},... | collective-permute-start | bytes 3145736 | tf_op jit(solution)/shard_map/ppermute | solution.py:21
  12.9 163.7 %collective-permute-start.19 = (bf16[256,2048]{0,1:T(8,128)(2,1)S(1)}, bf16[256,2048]{0,1:T(8,128)(2,1)S(1)}, u32[]{:S(2)}, u32[]{:S(2)}) collective-permute-start(bf16[256,2048]{0,1:T(8,128)(2,1)S(1)} %copy.34), channel_id=1, source_target_pairs={{0,5},{1,6},{2,7},{3,8},{4,9},{5,10},{6,11},{7,12},{8,13},{9,14},{... | collective-permute-start | bytes 3145736 | tf_op jit(solution)/shard_map/ppermute | solution.py:21
  16.2 11.7 %collective-permute-start.25 = (s32[3]{0:T(128)S(1)}, s32[3]{0:T(128)S(1)}, u32[]{:S(2)}, u32[]{:S(2)}) collective-permute-start(s32[3]{0:T(128)S(1)} %slice.62), channel_id=1, source_target_pairs={{0,1},{1,2},{2,3},{3,4},{4,5},{5,6},{6,7},{7,8},{8,9},{9,10},{10,1... | collective-permute-start | bytes 44 | tf_op jit(solution)/shard_map/ppermute | solution.py:21
  27.9 58.4 %collective-permute-start.8 = (s32[256]{0:T(256)}, s32[256]{0:T(256)S(1)}, u32[]{:S(2)}, u32[]{:S(2)}) collective-permute-start(s32[256]{0:T(256)} %param.17), channel_id=1, source_target_pairs={{0,8},{1,9},{2,10},{3,11},{4,12},{5,13},{6,14},{7,15},{8,16},{9,17... | collective-permute-start | bytes 3080 | tf_op jit(solution)/shard_map/ppermute | solution.py:21
  86.3 12.0 %collective-permute-start.9 = (s32[256]{0:T(256)}, s32[256]{0:T(256)S(1)}, u32[]{:S(2)}, u32[]{:S(2)}) collective-permute-start(s32[256]{0:T(256)} %param.17), channel_id=1, source_target_pairs={{0,7},{1,8},{2,9},{3,10},{4,11},{5,12},{6,13},{7,14},{8,15},{9,16}... | collective-permute-start | bytes 3080 | tf_op jit(solution)/shard_map/ppermute | solution.py:21
  98.4 7.1 %collective-permute-start.10 = (s32[256]{0:T(256)}, s32[256]{0:T(256)S(1)}, u32[]{:S(2)}, u32[]{:S(2)}) collective-permute-start(s32[256]{0:T(256)} %param.17), channel_id=1, source_target_pairs={{0,6},{1,7},{2,8},{3,9},{4,10},{5,11},{6,12},{7,13},{8,14},{9,15},... | collective-permute-start | bytes 3080 | tf_op jit(solution)/shard_map/ppermute | solution.py:21
  105.5 7.1 %collective-permute-start.11 = (s32[256]{0:T(256)}, s32[256]{0:T(256)S(1)}, u32[]{:S(2)}, u32[]{:S(2)}) collective-permute-start(s32[256]{0:T(256)} %param.17), channel_id=1, source_target_pairs={{0,5},{1,6},{2,7},{3,8},{4,9},{5,10},{6,11},{7,12},{8,13},{9,14},{... | collective-permute-start | bytes 3080 | tf_op jit(solution)/shard_map/ppermute | solution.py:21
  112.7 8.1 %collective-permute-start.12 = (s32[256]{0:T(256)}, s32[256]{0:T(256)S(1)}, u32[]{:S(2)}, u32[]{:S(2)}) collective-permute-start(s32[256]{0:T(256)} %param.17), channel_id=1, source_target_pairs={{0,4},{1,5},{2,6},{3,7},{4,8},{5,9},{6,10},{7,11},{8,12},{9,13},{1... | collective-permute-start | bytes 3080 | tf_op jit(solution)/shard_map/ppermute | solution.py:21
  120.7 7.5 %collective-permute-start.13 = (s32[256]{0:T(256)}, s32[256]{0:T(256)S(1)}, u32[]{:S(2)}, u32[]{:S(2)}) collective-permute-start(s32[256]{0:T(256)} %param.17), channel_id=1, source_target_pairs={{0,3},{1,4},{2,5},{3,6},{4,7},{5,8},{6,9},{7,10},{8,11},{9,12},{10... | collective-permute-start | bytes 3080 | tf_op jit(solution)/shard_map/ppermute | solution.py:21
  128.2 7.8 %collective-permute-start.14 = (s32[256]{0:T(256)}, s32[256]{0:T(256)S(1)}, u32[]{:S(2)}, u32[]{:S(2)}) collective-permute-start(s32[256]{0:T(256)} %param.17), channel_id=1, source_target_pairs={{0,2},{1,3},{2,4},{3,5},{4,6},{5,7},{6,8},{7,9},{8,10},{9,11},{10,... | collective-permute-start | bytes 3080 | tf_op jit(solution)/shard_map/ppermute | solution.py:21
  136.0 7.2 %collective-permute-start.15 = (s32[256]{0:T(256)}, s32[256]{0:T(256)S(1)}, u32[]{:S(2)}, u32[]{:S(2)}) collective-permute-start(s32[256]{0:T(256)} %param.17), channel_id=1, source_target_pairs={{0,1},{1,2},{2,3},{3,4},{4,5},{5,6},{6,7},{7,8},{8,9},{9,10},{10,1... | collective-permute-start | bytes 3080 | tf_op jit(solution)/shard_map/ppermute | solution.py:21
  143.2 7.3 %collective-permute-start.26 = (bf16[3,4096]{1,0:T(4,128)(2,1)S(1)}, bf16[3,4096]{1,0:T(4,128)(2,1)S(1)}, u32[]{:S(2)}, u32[]{:S(2)}) collective-permute-start(bf16[3,4096]{1,0:T(4,128)(2,1)S(1)} %slice.65), channel_id=1, source_target_pairs={{0,1},{1,2},{2,3},{3,4},{4,5},{5,6},{6,7},{7,8},{8,9},{9,10},{10,1... | collective-permute-start | bytes 73736 | tf_op jit(solution)/shard_map/ppermute | solution.py:21
  150.5 30.4 %collective-permute-start.20 = (bf16[256,2048]{0,1:T(8,128)(2,1)S(1)}, bf16[256,2048]{0,1:T(8,128)(2,1)S(1)}, u32[]{:S(2)}, u32[]{:S(2)}) collective-permute-start(bf16[256,2048]{0,1:T(8,128)(2,1)S(1)} %copy.34), channel_id=1, source_target_pairs={{0,4},{1,5},{2,6},{3,7},{4,8},{5,9},{6,10},{7,11},{8,12},{9,13},{1... | collective-permute-start | bytes 3145736 | tf_op jit(solution)/shard_map/ppermute | solution.py:21
  161.2 23.0 %copy-start.2 = (bf16[256,4096]{1,0:T(8,128)(2,1)}, bf16[256,4096]{1,0:T(8,128)(2,1)S(1)}, u32[]{:S(2)}) copy-start(bf16[256,4096]{1,0:T(8,128)(2,1)S(1)} %multiply_convert_fusion) | copy-start | bytes 6291460
  162.5 33.0 %collective-permute-start.21 = (bf16[256,2048]{0,1:T(8,128)(2,1)S(1)}, bf16[256,2048]{0,1:T(8,128)(2,1)S(1)}, u32[]{:S(2)}, u32[]{:S(2)}) collective-permute-start(bf16[256,2048]{0,1:T(8,128)(2,1)S(1)} %copy.34), channel_id=1, source_target_pairs={{0,3},{1,4},{2,5},{3,6},{4,7},{5,8},{6,9},{7,10},{8,11},{9,12},{10... | collective-permute-start | bytes 3145736 | tf_op jit(solution)/shard_map/ppermute | solution.py:21
  165.7 111.1 %collective-permute-start.22 = (bf16[256,2048]{0,1:T(8,128)(2,1)S(1)}, bf16[256,2048]{0,1:T(8,128)(2,1)S(1)}, u32[]{:S(2)}, u32[]{:S(2)}) collective-permute-start(bf16[256,2048]{0,1:T(8,128)(2,1)S(1)} %copy.34), channel_id=1, source_target_pairs={{0,2},{1,3},{2,4},{3,5},{4,6},{5,7},{6,8},{7,9},{8,10},{9,11},{10,... | collective-permute-start | bytes 3145736 | tf_op jit(solution)/shard_map/ppermute | solution.py:21
  168.9 109.9 %collective-permute-start.23 = (bf16[256,2048]{0,1:T(8,128)(2,1)S(1)}, bf16[256,2048]{0,1:T(8,128)(2,1)S(1)}, u32[]{:S(2)}, u32[]{:S(2)}) collective-permute-start(bf16[256,2048]{0,1:T(8,128)(2,1)S(1)} %copy.34), channel_id=1, source_target_pairs={{0,1},{1,2},{2,3},{3,4},{4,5},{5,6},{6,7},{7,8},{8,9},{9,10},{10,1... | collective-permute-start | bytes 3145736 | tf_op jit(solution)/shard_map/ppermute | solution.py:21
  176.7 156.4 %collective-permute-start = (bf16[256,2048]{0,1:T(8,128)(2,1)S(1)}, bf16[256,2048]{0,1:T(8,128)(2,1)S(1)}, u32[]{:S(2)}, u32[]{:S(2)}) collective-permute-start(bf16[256,2048]{0,1:T(8,128)(2,1)S(1)} %copy.25), channel_id=1, source_target_pairs={{0,8},{1,9},{2,10},{3,11},{4,12},{5,13},{6,14},{7,15},{8,16},{9,17... | collective-permute-start | bytes 3145736 | tf_op jit(solution)/shard_map/ppermute | solution.py:21
  181.0 185.7 %collective-permute-start.1 = (bf16[256,2048]{0,1:T(8,128)(2,1)S(1)}, bf16[256,2048]{0,1:T(8,128)(2,1)S(1)}, u32[]{:S(2)}, u32[]{:S(2)}) collective-permute-start(bf16[256,2048]{0,1:T(8,128)(2,1)S(1)} %copy.25), channel_id=1, source_target_pairs={{0,7},{1,8},{2,9},{3,10},{4,11},{5,12},{6,13},{7,14},{8,15},{9,16}... | collective-permute-start | bytes 3145736 | tf_op jit(solution)/shard_map/ppermute | solution.py:21
  195.4 173.2 %collective-permute-start.2 = (bf16[256,2048]{0,1:T(8,128)(2,1)S(1)}, bf16[256,2048]{0,1:T(8,128)(2,1)S(1)}, u32[]{:S(2)}, u32[]{:S(2)}) collective-permute-start(bf16[256,2048]{0,1:T(8,128)(2,1)S(1)} %copy.25), channel_id=1, source_target_pairs={{0,6},{1,7},{2,8},{3,9},{4,10},{5,11},{6,12},{7,13},{8,14},{9,15},... | collective-permute-start | bytes 3145736 | tf_op jit(solution)/shard_map/ppermute | solution.py:21
  276.8 93.9 %collective-permute-start.3 = (bf16[256,2048]{0,1:T(8,128)(2,1)S(1)}, bf16[256,2048]{0,1:T(8,128)(2,1)S(1)}, u32[]{:S(2)}, u32[]{:S(2)}) collective-permute-start(bf16[256,2048]{0,1:T(8,128)(2,1)S(1)} %copy.25), channel_id=1, source_target_pairs={{0,5},{1,6},{2,7},{3,8},{4,9},{5,10},{6,11},{7,12},{8,13},{9,14},{... | collective-permute-start | bytes 3145736 | tf_op jit(solution)/shard_map/ppermute | solution.py:21
  278.8 97.9 %collective-permute-start.4 = (bf16[256,2048]{0,1:T(8,128)(2,1)S(1)}, bf16[256,2048]{0,1:T(8,128)(2,1)S(1)}, u32[]{:S(2)}, u32[]{:S(2)}) collective-permute-start(bf16[256,2048]{0,1:T(8,128)(2,1)S(1)} %copy.25), channel_id=1, source_target_pairs={{0,4},{1,5},{2,6},{3,7},{4,8},{5,9},{6,10},{7,11},{8,12},{9,13},{1... | collective-permute-start | bytes 3145736 | tf_op jit(solution)/shard_map/ppermute | solution.py:21
  280.9 96.0 %copy-start = (bf16[2304,2048]{0,1:T(8,128)(2,1)}, bf16[2304,2048]{0,1:T(8,128)(2,1)S(1)}, u32[]{:S(2)}) copy-start(bf16[2304,2048]{0,1:T(8,128)(2,1)S(1)} %constant_dynamic-update-slice_fusion.11) | copy-start | bytes 28311556
  333.1 43.8 %collective-permute-start.5 = (bf16[256,2048]{0,1:T(8,128)(2,1)S(1)}, bf16[256,2048]{0,1:T(8,128)(2,1)S(1)}, u32[]{:S(2)}, u32[]{:S(2)}) collective-permute-start(bf16[256,2048]{0,1:T(8,128)(2,1)S(1)} %copy.25), channel_id=1, source_target_pairs={{0,3},{1,4},{2,5},{3,6},{4,7},{5,8},{6,9},{7,10},{8,11},{9,12},{10... | collective-permute-start | bytes 3145736 | tf_op jit(solution)/shard_map/ppermute | solution.py:21
  366.7 30.0 %collective-permute-start.6 = (bf16[256,2048]{0,1:T(8,128)(2,1)S(1)}, bf16[256,2048]{0,1:T(8,128)(2,1)S(1)}, u32[]{:S(2)}, u32[]{:S(2)}) collective-permute-start(bf16[256,2048]{0,1:T(8,128)(2,1)S(1)} %copy.25), channel_id=1, source_target_pairs={{0,2},{1,3},{2,4},{3,5},{4,6},{5,7},{6,8},{7,9},{8,10},{9,11},{10,... | collective-permute-start | bytes 3145736 | tf_op jit(solution)/shard_map/ppermute | solution.py:21
  368.7 37.4 %collective-permute-start.7 = (bf16[256,2048]{0,1:T(8,128)(2,1)S(1)}, bf16[256,2048]{0,1:T(8,128)(2,1)S(1)}, u32[]{:S(2)}, u32[]{:S(2)}) collective-permute-start(bf16[256,2048]{0,1:T(8,128)(2,1)S(1)} %copy.25), channel_id=1, source_target_pairs={{0,1},{1,2},{2,3},{3,4},{4,5},{5,6},{6,7},{7,8},{8,9},{9,10},{10,1... | collective-permute-start | bytes 3145736 | tf_op jit(solution)/shard_map/ppermute | solution.py:21
  370.7 39.1 %copy-start.7 = (s32[256]{0:T(256)S(1)}, s32[256]{0:T(256)}, u32[]{:S(2)}) copy-start(s32[256]{0:T(256)} %param.17) | copy-start | bytes 3076
  370.7 39.1 %copy-start.9 = (s32[2]{0:T(128)S(1)}, s32[2]{0:T(128)}, u32[]{:S(2)}) copy-start(s32[2]{0:T(128)} %param.18) | copy-start | bytes 28
  370.7 129.7 %collective-permute-start.27 = (bf16[128,4096]{1,0:T(8,128)(2,1)}, bf16[128,4096]{1,0:T(8,128)(2,1)}, u32[]{:S(2)}, u32[]{:S(2)}) collective-permute-start(bf16[128,4096]{1,0:T(8,128)(2,1)} %slice.80), channel_id=1, source_target_pairs={{1,0},{2,1},{3,2},{4,3},{5,4},{6,5},{7,6},{8,7},{9,8},{10,9},{11,1... | collective-permute-start | bytes 3145736 | tf_op jit(solution)/shard_map/ppermute | solution.py:21
  406.2 3.6 copy-start.1
  409.8 90.6 %copy-start.3 = (bf16[256,4096]{1,0:T(8,128)(2,1)S(1)}, bf16[256,4096]{1,0:T(8,128)(2,1)}, u32[]{:S(2)}) copy-start(bf16[256,4096]{1,0:T(8,128)(2,1)} %copy-done.2) | copy-start | bytes 6291460
  409.8 90.6 %copy-start.6 = (bf16[384]{0:T(512)(128)(2,1)S(1)}, bf16[384]{0:T(512)(128)(2,1)}, u32[]{:S(2)}) copy-start(bf16[384]{0:T(512)(128)(2,1)} %pad_dynamic-slice_fusion.4) | copy-start | bytes 2308
  409.8 90.6 %copy-start.8 = (pred[384]{0:T(512)(128)(4,1)S(1)}, pred[384]{0:T(512)(128)(4,1)}, u32[]{:S(2)}) copy-start(pred[384]{0:T(512)(128)(4,1)} %iota_compare_fusion) | copy-start | bytes 1156
  415.1 12.1 %copy-start.4 = (bf16[256,2048]{1,0:T(8,128)(2,1)S(1)}, bf16[256,2048]{1,0:T(8,128)(2,1)}, u32[]{:S(2)}) copy-start(bf16[256,2048]{1,0:T(8,128)(2,1)} %get-tuple-element.349) | copy-start | bytes 3145732 | tf_op jit(solution)/shard_map/while
  458.8 12.1 %copy-start.4 = (bf16[256,2048]{1,0:T(8,128)(2,1)S(1)}, bf16[256,2048]{1,0:T(8,128)(2,1)}, u32[]{:S(2)}) copy-start(bf16[256,2048]{1,0:T(8,128)(2,1)} %get-tuple-element.349) | copy-start | bytes 3145732 | tf_op jit(solution)/shard_map/while
  497.3 10.0 %copy-start.5 = (bf16[2,128,2048]{2,1,0:T(8,128)(2,1)S(1)}, bf16[2,128,2048]{2,1,0:T(8,128)(2,1)}, u32[]{:S(2)}) copy-start(bf16[2,128,2048]{2,1,0:T(8,128)(2,1)} %get-tuple-element.171) | copy-start | bytes 3145732
  498.4 8.8 %collective-permute-start.24 = (bf16[128,2048]{1,0:T(8,128)(2,1)S(1)}, bf16[128,2048]{1,0:T(8,128)(2,1)S(1)}, u32[]{:S(2)}, u32[]{:S(2)}) collective-permute-start(bf16[128,2048]{1,0:T(8,128)(2,1)S(1)} %slice_bitcast_fusion), channel_id=1, source_target_pairs={{1,0},{2,1},{3,2},{4,3},{5,4},{6,5},{7,6},{8,7},{9,8},{10,9},{11,1... | collective-permute-start | bytes 1572872 | tf_op jit(solution)/shard_map/ppermute | solution.py:21
where the time goes:
time: 514 us; the launch traced here: 509 us
  waiting for transfers between devices  266 us (52%)
  starting transfers between devices  113 us (22%)
  local copies, waits for them, and re-layouts  50.3 us (10%)
  matrix products  50 us (10%)
  other arithmetic  21.7 us (4%)
  loops' own time  6.56 us (1%)
    ppermute x28, waiting for transfers between devices, from_behind(): return lax.ppermute(block, axis, route)  266 us
    ppermute x28, starting transfers between devices, from_behind(): return lax.ppermute(block, axis, route)  113 us
    sub x2, matrix products, attend(): lifted = jnp.where(allowed[None], jnp.exp(scores - row_top), 0.0)  27.3 us
    dynamic_slice x2, local copies, waits for them, and re-layouts, own_block(): lax.dynamic_slice_in_dim(key_buffer, key_at, WINDOW + BLOCK, 0)  24.1 us
    dot_general x2, matrix products, attend(): jnp.einsum('hqk,khd->qhd', weights, heads_v, preferred_element_type=jnp.f...  22.8 us
    unnamed x44, local copies, waits for them, and re-layouts  11.4 us
  transfers between devices with their start and end apart: 28, of which 16 were waited for; matrix products, arithmetic and copies ran while one was open for 23% of the time, Pallas kernels for 0%

commit v1 on v0

v1 whole, which is shorter than its diff:
```python
import functools
import math

import jax
import jax.numpy as jnp
from jax import lax
from jax.experimental import pallas as pl
from jax.experimental.pallas import tpu as pltpu
from jax.sharding import PartitionSpec as P

HEADS = 16
D_HEAD = 128
WINDOW = 2048
BLOCK = 128
HALF = BLOCK // 2
KERNEL = 4
N = 32
ROWS = 256
SLOTS = 3
MSG = 3 * BLOCK + 8
TILES = N // 2
WIDTHS = (4, 6, 8, 10)
EXP_SCALE = math.log2(math.e) / math.sqrt(D_HEAD)
MASKED = -1e30
GROUP = 4


def pack_kernel(reach_ref, seg_ref, q_ref, k_ref, v_ref, out_ref):
    seg = seg_ref[...]
    lane = lax.broadcasted_iota(jnp.int32, (8, 128), 1)
    meta = jnp.zeros((8, 128), jnp.int32)
    for v in range(3):
        count = jnp.sum((seg <= v).astype(jnp.int32))
        meta = jnp.where(lane == v, count, meta)
    for b in range(2):
        reach = reach_ref[b]
        meta = jnp.where(lane == 3 + 2 * b, reach // 16, meta)
        meta = jnp.where(lane == 4 + 2 * b, reach % 16, meta)
    meta = meta.astype(jnp.float32).astype(jnp.bfloat16)
    for h in range(GROUP):
        for c in range(2):
            for n, ref in enumerate((q_ref, k_ref, v_ref)):
                for b in range(2):
                    at = b * BLOCK + c * HALF
                    out_ref[2 * h + c, n * BLOCK + b * HALF : n * BLOCK + (b + 1) * HALF, :] = ref[
                        at : at + HALF, h * D_HEAD : (h + 1) * D_HEAD
                    ]
            out_ref[2 * h + c, 3 * BLOCK :, :] = meta


def pack(q, k, v, seg, reach):
    wide = pl.BlockSpec((ROWS, GROUP * D_HEAD), lambda g: (0, g))
    return pl.pallas_call(
        pack_kernel,
        grid=(HEADS // GROUP,),
        in_specs=[
            pl.BlockSpec(memory_space=pltpu.SMEM),
            pl.BlockSpec((2, 128), lambda g: (0, 0)),
            wide,
            wide,
            wide,
        ],
        out_specs=pl.BlockSpec((2 * GROUP, MSG, D_HEAD), lambda g: (g, 0, 0)),
        out_shape=jax.ShapeDtypeStruct((N, MSG, D_HEAD), jnp.bfloat16),
        name="pack",
    )(reach, seg.reshape(2, 128), q, k, v)


def attend_kernel(core_ref, counts_ref, mine_ref, theirs_ref, out_ref, bounds_ref, s_ref, slot_ref, kmin_ref):
    core = core_ref[0]

    def fill(e, first):
        count = counts_ref[e]
        for j in range(SLOTS):
            slot_ref[first + j] = SLOTS * e + j
        return first + count

    lax.fori_loop(0, N, fill, jnp.int32(0))
    out_ref[...] = jnp.zeros_like(out_ref)

    meta = mine_ref[:, 3 * BLOCK, :].astype(jnp.float32).astype(jnp.int32)
    totals = jnp.sum(meta, axis=0, keepdims=True)
    bounds = [totals[:, v : v + 1] for v in range(3)]
    lane1 = lax.broadcasted_iota(jnp.int32, (1, 128), 1)
    for v in range(3):
        bounds_ref[v] = jnp.sum(jnp.where(lane1 == v, totals, 0))

    def lowest(t, first, reach):
        lo = jnp.maximum(t - (WINDOW - 1), first - reach)
        lo = jnp.maximum(lo, 0)
        for bound in bounds:
            lo = jnp.maximum(lo, jnp.where(bound <= t, bound, 0))
        return lo

    source = lax.broadcasted_iota(jnp.int32, (N, 1), 0)
    reaches = [meta[:, 3 + 2 * b : 4 + 2 * b] * 16 + meta[:, 4 + 2 * b : 5 + 2 * b] for b in range(2)]
    firsts = [source * ROWS + b * BLOCK for b in range(2)]
    least = jnp.minimum(
        lowest(firsts[0], firsts[0], reaches[0]), lowest(firsts[1], firsts[1], reaches[1])
    )
    for i in range(TILES):
        kmin_ref[i] = jnp.min(jnp.where(source // 2 == i, least, 1 << 20))

    col = lax.broadcasted_iota(jnp.int32, (1, 256), 1)
    col = (
        (col % 128) // HALF * BLOCK
        + col % HALF
        + jnp.where(col < 128, core, 1 - core) * HALF
    )
    row = lax.broadcasted_iota(jnp.int32, (HALF, 1), 0) + core * HALF
    ones = jnp.ones((256, D_HEAD), jnp.bfloat16)

    def tile(i, width):
        q = jnp.concatenate([mine_ref[2 * i, :BLOCK, :], mine_ref[2 * i + 1, :BLOCK, :]], axis=0)
        times, lows = [], []
        for part in range(4):
            first = i * (2 * ROWS) + part * BLOCK
            t = first + row
            figures = mine_ref[2 * i + part // 2, 3 * BLOCK :, :].astype(jnp.float32).astype(jnp.int32)
            at = 3 + 2 * (part % 2)
            reach = figures[:1, at : at + 1] * 16 + figures[:1, at + 1 : at + 2]
            times.append(t)
            lows.append(lowest(t, first, reach))
        time = jnp.concatenate(times, axis=0)
        low = jnp.concatenate(lows, axis=0)
        start = 2 * i + 2 - width
        top = None
        for w in range(width):
            j = start + w
            held = jnp.maximum(j, 0)
            k = jnp.concatenate(
                [mine_ref[held, BLOCK : 2 * BLOCK, :], theirs_ref[held, BLOCK : 2 * BLOCK, :]], axis=0
            )
            s = lax.dot_general(q, k, (((1,), (1,)), ((), ())), preferred_element_type=jnp.float32)
            pos = col + j * ROWS
            allowed = pos >= low
            if w >= width - 2:
                allowed = allowed & (pos <= time)
            s = jnp.where(allowed, s, MASKED)
            s_ref[:, w * 256 : (w + 1) * 256] = s
            here = jnp.maximum(s[:, :128], s[:, 128:])
            top = here if top is None else jnp.maximum(top, here)
        top = jnp.max(top, axis=1, keepdims=True) * EXP_SCALE
        acc = None
        for w in range(width):
            held = jnp.maximum(start + w, 0)
            p = jnp.exp2(s_ref[:, w * 256 : (w + 1) * 256] * EXP_SCALE - top).astype(jnp.bfloat16)
            v = jnp.concatenate(
                [mine_ref[held, 2 * BLOCK : 3 * BLOCK, :], theirs_ref[held, 2 * BLOCK : 3 * BLOCK, :]], axis=0
            )
            v = jnp.concatenate([v, ones], axis=1)
            o = lax.dot_general(p, v, (((1,), (0,)), ((), ())), preferred_element_type=jnp.float32)
            acc = o if acc is None else acc + o
        o = (acc[:, :D_HEAD] / acc[:, D_HEAD:]).astype(jnp.bfloat16)
        for part in range(4):
            out_ref[slot_ref[4 * i + part]] = o[part * HALF : (part + 1) * HALF]

    def step(i, carry):
        need = 2 * i + 2 - kmin_ref[i] // ROWS
        below = 0
        for width in WIDTHS:
            @pl.when((need > below) & (need <= width))
            def _(width=width):
                tile(i, width)

            below = width
        return carry

    lax.fori_loop(0, TILES, step, 0)


def attention(mine, theirs, core, counts):
    smem = pl.BlockSpec(memory_space=pltpu.SMEM)
    vmem = pl.BlockSpec(memory_space=pltpu.VMEM)
    return pl.pallas_call(
        attend_kernel,
        in_specs=[smem, smem, vmem, vmem],
        out_specs=(vmem, smem),
        out_shape=(
            jax.ShapeDtypeStruct((N * SLOTS, HALF, D_HEAD), jnp.bfloat16),
            jax.ShapeDtypeStruct((4,), jnp.int32),
        ),
        scratch_shapes=[
            pltpu.VMEM((256, 256 * max(WIDTHS)), jnp.float32),
            pltpu.SMEM((2 * N + 8,), jnp.int32),
            pltpu.SMEM((TILES,), jnp.int32),
        ],
        cost_estimate=pl.CostEstimate(
            flops=10 * 10**9, bytes_accessed=8 * 2**20, transcendentals=10**7
        ),
        name="attend",
    )(core, counts, mine, theirs)


def gather_kernel(in_ref, out_ref):
    for h in range(HEADS):
        for c in range(2):
            out_ref[c * HALF : (c + 1) * HALF, h * D_HEAD : (h + 1) * D_HEAD] = in_ref[2 * h + c]


def assemble(received):
    return pl.pallas_call(
        gather_kernel,
        grid=(SLOTS,),
        in_specs=[pl.BlockSpec((N, HALF, D_HEAD), lambda j: (0, j, 0))],
        out_specs=pl.BlockSpec((BLOCK, HEADS * D_HEAD), lambda j: (j, 0)),
        out_shape=jax.ShapeDtypeStruct((SLOTS * BLOCK, HEADS * D_HEAD), jnp.bfloat16),
        name="assemble",
    )(received)


def conv_kernel(figures_ref, bounds_ref, inner_ref, next_ref, tail_ref, weight_ref, bias_ref, out_ref, ext_ref):
    index, off, count = figures_ref[0], figures_ref[1], figures_ref[2]
    ext_ref[:8, :] = tail_ref[...].astype(jnp.float32)
    ext_ref[8 : 8 + ROWS, :] = inner_ref[...].astype(jnp.float32)
    ext_ref[8 + ROWS :, :] = next_ref[...].astype(jnp.float32)
    for block in range(SLOTS):
        slot = block - off

        @pl.when((slot >= 0) & (slot < count))
        def _(block=block, slot=slot):
            time = index * ROWS + block * BLOCK + lax.broadcasted_iota(jnp.int32, (BLOCK, 1), 0)
            start = jnp.zeros_like(time)
            for v in range(3):
                start = jnp.maximum(start, jnp.where(bounds_ref[v] <= time, bounds_ref[v], 0))
            since = time - start
            at = 8 + block * BLOCK
            total = bias_ref[...] + weight_ref[0:1, :] * ext_ref[at : at + BLOCK, :]
            for j in range(1, KERNEL):
                row = jnp.where(since >= j, ext_ref[at - j : at - j + BLOCK, :], 0.0)
                total = total + weight_ref[j : j + 1, :] * row
            out_ref[pl.ds(pl.multiple_of(slot * BLOCK, BLOCK), BLOCK), :] = (
                total / (1.0 + jnp.exp(-total))
            ).astype(jnp.bfloat16)

    for slot in range(1, SLOTS):

        @pl.when(slot >= count)
        def _(slot=slot):
            out_ref[slot * BLOCK : (slot + 1) * BLOCK, :] = jnp.zeros((BLOCK, out_ref.shape[1]), jnp.bfloat16)


def convolve(figures, bounds, inner, following, tail, weight, bias):
    channels = inner.shape[1]
    width = 512
    smem = pl.BlockSpec(memory_space=pltpu.SMEM)

    def wide(rows):
        return pl.BlockSpec((rows, width), lambda g: (0, g))

    return pl.pallas_call(
        conv_kernel,
        grid=(channels // width,),
        in_specs=[smem, smem, wide(ROWS), wide(BLOCK), wide(8), wide(KERNEL), wide(1)],
        out_specs=wide(SLOTS * BLOCK),
        out_shape=jax.ShapeDtypeStruct((SLOTS * BLOCK, channels), jnp.bfloat16),
        scratch_shapes=[pltpu.VMEM((8 + ROWS + BLOCK, width), jnp.float32)],
        cost_estimate=pl.CostEstimate(
            flops=10 * 10**9, bytes_accessed=6 * 2**20, transcendentals=2 * 10**6
        ),
        name="conv",
    )(figures, bounds, inner, following, tail, weight, bias.reshape(1, -1))


def shards(queries, key_rows, values, inner_rows, conv_weight, conv_bias, segment_ids, block_reach, owner_counts):
    index = lax.axis_index("ctx").astype(jnp.int32)
    places = jnp.arange(N, dtype=jnp.int32)
    first = jnp.sum(jnp.where(places < index, owner_counts, 0))
    count = jnp.sum(jnp.where(places == index, owner_counts, 0))
    figures = jnp.stack([index, first - 2 * index, count, index])

    sent = pack(queries, key_rows, values, segment_ids, block_reach)
    mine = lax.all_to_all(sent, "ctx", 0, 0, tiled=True)
    theirs = lax.ppermute(mine, "ctx", [(i, i ^ 1) for i in range(N)])
    following = lax.ppermute(inner_rows[:BLOCK], "ctx", [(i, i - 1) for i in range(1, N)])
    tail = lax.ppermute(inner_rows[ROWS - 8 :], "ctx", [(i, i + 1) for i in range(N - 1)])
    out, bounds = attention(mine, theirs, (index % 2).reshape(1), owner_counts)
    received = lax.all_to_all(out.reshape(N, SLOTS * HALF, D_HEAD), "ctx", 0, 0, tiled=True)
    attn_owned = assemble(received)
    conv_owned = convolve(figures, bounds, inner_rows, following, tail, conv_weight, conv_bias)
    return attn_owned, conv_owned


def solution(mesh):
    rows = P(("dp", "ctx"), None)
    flat = P(("dp", "ctx"))
    return jax.shard_map(
        shards,
        mesh=mesh,
        in_specs=(rows, rows, rows, rows, P(), P(), flat, flat, P("dp")),
        out_specs=(rows, rows),
        check_vma=False,
    )
```

time: 514 us -> 127 us (0.25)
  waiting for transfers between devices: 266 us -> 16.1 us
  starting transfers between devices: 113 us -> 11.4 us
  matrix products: 50 us -> 0 us
  blocking collectives: 0 us -> 47.5 us
  local copies, waits for them, and re-layouts: 50.3 us -> 3.84 us
  Pallas kernels: 0 us -> 43.4 us
  other arithmetic: 21.7 us -> 2.02 us
  loops' own time: 6.56 us -> 0 us
    ppermute x28 -> x3, waiting for transfers between devices: 266 us -> 16.1 us  [the longest x1 15.7 us: shards(): lax.ppermute(inner_rows[ROWS - 8:], 'ctx', [(i, i + 1) for i in range(N -...]
    ppermute x28 -> x3, starting transfers between devices: 113 us -> 6.28 us  [the longest x1 4.15 us: shards(): lax.ppermute(inner_rows[:BLOCK], 'ctx', [(i, i - 1) for i in range(1, N)])]
    all_to_all x0 -> x1, blocking collectives: none -> 47.5 us  [shards(): mine = lax.all_to_all(sent, 'ctx', 0, 0, tiled=True)]
    pallas_call x0 -> x4, Pallas kernels: none -> 43.4 us  [the longest x1 25.7 us: attention(): pl.pallas_call(attend_kernel, in_specs=[smem, smem, vmem, vmem], out_spec...]
    dynamic_slice x17 -> x0, local copies, waits for them, and re-layouts: 30.2 us -> none  [the longest x2 24.1 us: own_block(): lax.dynamic_slice_in_dim(key_buffer, key_at, WINDOW + BLOCK, 0)]
    sub x2 -> x0, matrix products: 27.3 us -> none  [attend(): lifted = jnp.where(allowed[None], jnp.exp(scores - row_top), 0.0)]
    dot_general x2 -> x0, matrix products: 22.8 us -> none  [attend(): jnp.einsum('hqk,khd->qhd', weights, heads_v, preferred_element_type=jnp.f...]
    unnamed x44 -> x10, local copies, waits for them, and re-layouts: 11.4 us -> 1.79 us
  transfers between devices with their start and end apart: 28 -> 4, of which waited for: 16 -> 2; matrix products, arithmetic and copies ran while one was open for 23% -> 3% of each run, Pallas kernels for 0% -> 28%
where the time goes in v1:
time: 127 us; the launch traced here: 126 us
  blocking collectives  47.5 us (37%)
  Pallas kernels  43.4 us (34%)
  waiting for transfers between devices  16.1 us (13%)
  starting transfers between devices  11.4 us (9%)
  local copies, waits for them, and re-layouts  3.84 us (3%)
  other arithmetic  2.02 us (2%)
  between operations  1.39 us (1%)
    all_to_all x1, blocking collectives, shards(): mine = lax.all_to_all(sent, 'ctx', 0, 0, tiled=True)  47.5 us
    pallas_call x1, Pallas kernels, attention(): pl.pallas_call(attend_kernel, in_specs=[smem, smem, vmem, vmem], out_spec...  25.7 us
    ppermute x1, waiting for transfers between devices, shards(): lax.ppermute(inner_rows[ROWS - 8:], 'ctx', [(i, i + 1) for i in range(N -...  15.7 us
    pallas_call x1, Pallas kernels, convolve(): pl.pallas_call(conv_kernel, grid=(channels // width,), in_specs=[smem, sm...  9.71 us
    all_to_all x1, starting transfers between devices, shards(): lax.all_to_all(out.reshape(N, SLOTS * HALF, D_HEAD), 'ctx', 0, 0, tiled=T...  5.09 us
    pallas_call x1, Pallas kernels, pack(): pl.pallas_call(pack_kernel, grid=(HEADS // GROUP,), in_specs=[pl.BlockSpe...  4.4 us
    ppermute x1, starting transfers between devices, shards(): lax.ppermute(inner_rows[:BLOCK], 'ctx', [(i, i - 1) for i in range(1, N)])  4.15 us
    pallas_call x1, Pallas kernels, assemble(): pl.pallas_call(gather_kernel, grid=(SLOTS,), in_specs=[pl.BlockSpec((N, H...  3.55 us
  transfers between devices with their start and end apart: 4, of which 2 were waited for; matrix products, arithmetic and copies ran while one was open for 3% of the time, Pallas kernels for 28%

profile of v1, /device:TPU:104, one launch (start us, length us, event | category | flops | bytes accessed | tf_op | source)
XLA Modules:
  0.0 125.6 jit_solution(119522311224587085)
XLA Ops:
  0.6 4.4 %pack.1 = bf16[32,392,128]{2,1,0:T(8,128)(2,1)} custom-call(s32[2]{0:T(128)} %reach_ref.1, s32[2,128]{1,0:T(2,128)} %bitcast.8, bf16[256,2048]{1,0:T(8,128)(2,1)} %q_ref.1, bf16[256,2048]{1,0:T(8,128)(2,1)} %k_ref.1, bf16[256,2048]{1,0:T(8,128)(2,1)} %v_ref.1), custom_call_target="tpu_custom_call" | custom-call | tf_op jit(solution)/shard_map/pack/pallas_call | solution.py:53
  5.0 0.0 copy-start.2
  5.0 47.5 %all_to_all.10.mine_ref = bf16[32,392,128]{2,1,0:T(8,128)(2,1)S(1)} all-to-all(bf16[32,392,128]{2,1,0:T(8,128)(2,1)} %pack.1), channel_id=1, replica_groups=mesh['dp'=8,'ctx'=32] {'ctx'}, dimensions={0} | all-to-all | bytes 6422528 | tf_op jit(solution)/shard_map/all_to_all | solution.py:273
  52.5 0.0 copy-start.1
  52.5 0.1 collective-permute-start
  52.6 0.0 copy-done.2
  52.6 1.2 slice.6
  53.8 4.1 %collective-permute-start.1 = (bf16[128,4096]{1,0:T(8,128)(2,1)}, bf16[128,4096]{1,0:T(8,128)(2,1)}, u32[]{:S(2)}, u32[]{:S(2)}) collective-permute-start(bf16[128,4096]{1,0:T(8,128)(2,1)} %slice.6), channel_id=1, source_target_pairs={{1,0},{2,1},{3,2},{4,3},{5,4},{6,5},{7,6},{8,7},{9,8},{10,9},{11,1... | collective-permute-start | bytes 3145736 | tf_op jit(solution)/shard_map/ppermute | solution.py:275
  58.0 0.4 collective-permute-done.theirs_ref
  58.4 0.0 copy-done.1
  58.4 25.7 %attend.1 = (bf16[96,64,128]{2,1,0:T(8,128)(2,1)}, s32[4]{0:T(128)}) custom-call(s32[1]{0:T(128)} %bitcast.core_ref, s32[32]{0:T(128)} %counts_ref.1, bf16[32,392,128]{2,1,0:T(8,128)(2,1)} %copy-done.1, bf16[32,392,128]{2,1,0:T(8,128)(2,1)} %collective-permute-done.theirs_ref), custom_call_target="tpu_custom_call" | custom-call | flops 10000000000 | bytes 8388608 | tf_op jit(solution)/shard_map/attend/pallas_call | solution.py:175
  84.1 0.0 copy-start.3
  84.1 5.1 %all-to-all-start.1 = ((bf16[32,192,128]{2,1,0:T(8,128)(2,1)}), bf16[32,192,128]{2,1,0:T(8,128)(2,1)S(1)}, u32[]{:S(2)}, u32[]{:S(2)}) async-start(bf16[32,192,128]{2,1,0:T(8,128)(2,1)} %bitcast.7), calls=%async_computation.1 | async-start | bytes 3145728 | tf_op jit(solution)/shard_map/all_to_all | solution.py:278
  89.2 0.8 slice.7
  90.1 2.0 %collective-permute-start.2 = (bf16[8,4096]{1,0:T(8,128)(2,1)S(1)}, bf16[8,4096]{1,0:T(8,128)(2,1)S(1)}, u32[]{:S(2)}, u32[]{:S(2)}) collective-permute-start(bf16[8,4096]{1,0:T(8,128)(2,1)S(1)} %slice.7), channel_id=1, source_target_pairs={{0,1},{1,2},{2,3},{3,4},{4,5},{5,6},{6,7},{7,8},{8,9},{9,10},{10,1... | collective-permute-start | bytes 196616 | tf_op jit(solution)/shard_map/ppermute | solution.py:276
  92.1 0.0 copy-done.3
  92.1 0.7 fusion
  93.5 1.3 %pad_add_fusion.figures_ref = s32[4]{0:T(128)} fusion(s32[1]{0:T(128)} %bitcast.3, s32[1]{0:T(128)} %bitcast.5, s32[1]{0:T(128)} %bitcast.4), kind=kLoop, calls=%fused_computation.4 | loop fusion | flops 12 | bytes 28 | tf_op jit(solution)/shard_map/stack | solution.py:270
  94.8 15.7 %collective-permute-done.2.tail_ref = bf16[8,4096]{1,0:T(8,128)(2,1)S(1)} collective-permute-done((bf16[8,4096]{1,0:T(8,128)(2,1)S(1)}, bf16[8,4096]{1,0:T(8,128)(2,1)S(1)}, u32[]{:S(2)}, u32[]{:S(2)}) %collective-permute-start.2) | collective-permute-done | bytes 65568 | tf_op jit(solution)/shard_map/ppermute | solution.py:276
  110.5 0.0 copy-start.4
  110.5 0.0 collective-permute-done.1.next_ref
  110.5 0.6 copy-done.4
  111.2 9.7 %conv.1 = bf16[384,4096]{1,0:T(8,128)(2,1)} custom-call(s32[4]{0:T(128)} %pad_add_fusion.figures_ref, s32[4]{0:T(128)} %get-tuple-element.5.bounds_ref, bf16[256,4096]{1,0:T(8,128)(2,1)} %inner_ref.1, bf16[128,4096]{1,0:T(8,128)(2,1)} %collective-permute-done.1.next_ref, bf16[8,4096]{1,0:T(8,128)(2,1)} %copy-done.4, f32[4,4096]{1,0:T(4,128)} %weight_ref.1, ...), custom_call_target="tpu_custom_call" | custom-call | flops 10000000000 | bytes 6291456 | tf_op jit(solution)/shard_map/conv/pallas_call | solution.py:251
  120.9 0.0 all-to-all-done.1.in_ref
  120.9 0.0 copy-start
  120.9 1.1 copy-done
  122.0 3.5 %assemble.1 = bf16[384,2048]{1,0:T(8,128)(2,1)} custom-call(bf16[32,192,128]{2,1,0:T(8,128)(2,1)} %copy-done), custom_call_target="tpu_custom_call" | custom-call | tf_op jit(solution)/shard_map/assemble/pallas_call | solution.py:202
Async XLA Ops:
  5.0 47.6 %copy-start.2 = (bf16[256,4096]{1,0:T(8,128)(2,1)S(1)}, bf16[256,4096]{1,0:T(8,128)(2,1)}, u32[]{:S(2)}) copy-start(bf16[256,4096]{1,0:T(8,128)(2,1)} %inner_ref.1) | copy-start | bytes 6291460
  52.5 5.9 %copy-start.1 = (bf16[32,392,128]{2,1,0:T(8,128)(2,1)}, bf16[32,392,128]{2,1,0:T(8,128)(2,1)S(1)}, u32[]{:S(2)}) copy-start(bf16[32,392,128]{2,1,0:T(8,128)(2,1)S(1)} %all_to_all.10.mine_ref) | copy-start | bytes 9633796
  52.5 5.9 %collective-permute-start = (bf16[32,392,128]{2,1,0:T(8,128)(2,1)S(1)}, bf16[32,392,128]{2,1,0:T(8,128)(2,1)}, u32[]{:S(2)}, u32[]{:S(2)}) collective-permute-start(bf16[32,392,128]{2,1,0:T(8,128)(2,1)S(1)} %all_to_all.10.mine_ref), channel_id=1, source_target_pairs={{0,1},{1,0},{2,3},{3,2},{4,5},{5,4},{6,7},{7,6},{8,9},{9,8},{10,11... | collective-permute-start | bytes 9633800 | tf_op jit(solution)/shard_map/ppermute | solution.py:274
  53.8 56.7 %collective-permute-start.1 = (bf16[128,4096]{1,0:T(8,128)(2,1)}, bf16[128,4096]{1,0:T(8,128)(2,1)}, u32[]{:S(2)}, u32[]{:S(2)}) collective-permute-start(bf16[128,4096]{1,0:T(8,128)(2,1)} %slice.6), channel_id=1, source_target_pairs={{1,0},{2,1},{3,2},{4,3},{5,4},{6,5},{7,6},{8,7},{9,8},{10,9},{11,1... | collective-permute-start | bytes 3145736 | tf_op jit(solution)/shard_map/ppermute | solution.py:275
  84.1 8.0 %copy-start.3 = (s32[32]{0:T(128)S(1)}, s32[32]{0:T(128)}, u32[]{:S(2)}) copy-start(s32[32]{0:T(128)} %counts_ref.1) | copy-start | bytes 388
  84.1 36.7 %all-to-all-start.1 = ((bf16[32,192,128]{2,1,0:T(8,128)(2,1)}), bf16[32,192,128]{2,1,0:T(8,128)(2,1)S(1)}, u32[]{:S(2)}, u32[]{:S(2)}) async-start(bf16[32,192,128]{2,1,0:T(8,128)(2,1)} %bitcast.7), calls=%async_computation.1 | async-start | bytes 3145728 | tf_op jit(solution)/shard_map/all_to_all | solution.py:278
  90.1 20.4 %collective-permute-start.2 = (bf16[8,4096]{1,0:T(8,128)(2,1)S(1)}, bf16[8,4096]{1,0:T(8,128)(2,1)S(1)}, u32[]{:S(2)}, u32[]{:S(2)}) collective-permute-start(bf16[8,4096]{1,0:T(8,128)(2,1)S(1)} %slice.7), channel_id=1, source_target_pairs={{0,1},{1,2},{2,3},{3,4},{4,5},{5,6},{6,7},{7,8},{8,9},{9,10},{10,1... | collective-permute-start | bytes 196616 | tf_op jit(solution)/shard_map/ppermute | solution.py:276
  110.5 0.6 copy-start.4
  120.9 1.2 copy-start

commit v2 on v1

v2 whole, which is shorter than its diff:
```python
import functools
import math

import jax
import jax.numpy as jnp
from jax import lax
from jax.experimental import pallas as pl
from jax.experimental.pallas import tpu as pltpu
from jax.sharding import PartitionSpec as P

HEADS = 16
D_HEAD = 128
WINDOW = 2048
BLOCK = 128
HALF = BLOCK // 2
KERNEL = 4
N = 32
ROWS = 256
SLOTS = 3
MSG = 3 * BLOCK + 8
TILES = N // 2
WIDTH = 10
EXP_SCALE = math.log2(math.e) / math.sqrt(D_HEAD)
MASKED = -1e30
GROUP = 4


def pack_kernel(reach_ref, seg_ref, q_ref, k_ref, v_ref, out_ref, held_ref, sems):
    width = GROUP * D_HEAD
    copies = {}
    for g in range(HEADS // GROUP):
        for n, ref in enumerate((q_ref, k_ref, v_ref)):
            columns = pl.ds(g * width, width)
            copies[g, n] = pltpu.make_async_copy(
                ref.at[:, columns], held_ref.at[n, :, columns], sems.at[g, n]
            )
            copies[g, n].start()
    seg = seg_ref[...]
    lane = lax.broadcasted_iota(jnp.int32, (8, 128), 1)
    meta = jnp.zeros((8, 128), jnp.int32)
    for v in range(3):
        count = jnp.sum((seg <= v).astype(jnp.int32))
        meta = jnp.where(lane == v, count, meta)
    for b in range(2):
        reach = reach_ref[b]
        meta = jnp.where(lane == 3 + 2 * b, reach // 16, meta)
        meta = jnp.where(lane == 4 + 2 * b, reach % 16, meta)
    meta = meta.astype(jnp.float32).astype(jnp.bfloat16)
    for g in range(HEADS // GROUP):
        for n in range(3):
            copies[g, n].wait()
            for h in range(g * GROUP, (g + 1) * GROUP):
                for c in range(2):
                    if n == 2:
                        columns = slice(h * D_HEAD, (h + 1) * D_HEAD)
                        out_ref[2 * h + c, n * BLOCK : (n + 1) * BLOCK, :] = jnp.concatenate(
                            [
                                held_ref[n, at : at + HALF, columns]
                                for at in (c * HALF, BLOCK + c * HALF)
                            ],
                            axis=0,
                        ).T
                        continue
                    for b in range(2):
                        at = b * BLOCK + c * HALF
                        out_ref[2 * h + c, n * BLOCK + b * HALF : n * BLOCK + (b + 1) * HALF, :] = held_ref[
                            n, at : at + HALF, h * D_HEAD : (h + 1) * D_HEAD
                        ]
    for e in range(N):
        out_ref[e, 3 * BLOCK :, :] = meta


def pack(q, k, v, seg, reach):
    anywhere = pl.BlockSpec(memory_space=pl.ANY)
    vmem = pl.BlockSpec(memory_space=pltpu.VMEM)
    return pl.pallas_call(
        pack_kernel,
        in_specs=[pl.BlockSpec(memory_space=pltpu.SMEM), vmem, anywhere, anywhere, anywhere],
        out_specs=vmem,
        out_shape=pltpu.VMEM((N, MSG, D_HEAD), jnp.bfloat16),
        scratch_shapes=[
            pltpu.VMEM((3, ROWS, HEADS * D_HEAD), jnp.bfloat16),
            pltpu.SemaphoreType.DMA((HEADS // GROUP, 3)),
        ],
        compiler_params=pltpu.CompilerParams(vmem_limit_bytes=8 << 20),
        name="pack",
    )(in_hbm(reach), in_hbm(seg.reshape(2, 128)), in_hbm(q), in_hbm(k), in_hbm(v))


def attend_kernel(
    core_ref, counts_ref, mine_ref, theirs_ref, out_ref, bounds_ref,
    s0_ref, s1_ref, m0_ref, m1_ref, pos0_ref, pos1_ref, slot_ref,
):
    core = core_ref[0]

    def fill(e, first):
        count = counts_ref[e]
        for j in range(SLOTS):
            slot_ref[first + j] = SLOTS * e + j
        for j in range(1, SLOTS):

            @pl.when(count <= j)
            def _(j=j):
                out_ref[SLOTS * e + j] = jnp.zeros((HALF, D_HEAD), jnp.bfloat16)

        return first + count

    lax.fori_loop(0, N, fill, jnp.int32(0))

    meta = mine_ref[:, 3 * BLOCK, :].astype(jnp.float32).astype(jnp.int32)
    totals = jnp.sum(meta, axis=0, keepdims=True)
    bounds = [totals[:, v : v + 1] for v in range(3)]
    lane1 = lax.broadcasted_iota(jnp.int32, (1, 128), 1)
    for v in range(3):
        bounds_ref[v] = jnp.sum(jnp.where(lane1 == v, totals, 0))

    for ref in (pos0_ref, pos1_ref):
        key = lax.broadcasted_iota(jnp.int32, (2 * BLOCK, 128), 0)
        pos = (key % BLOCK) // HALF * BLOCK + key % HALF + jnp.where(key < BLOCK, core, 1 - core) * HALF
        for w in range(WIDTH):
            ref[w * 256 : (w + 1) * 256, :] = pos + w * ROWS
    ones = jnp.ones((16, 2 * BLOCK), jnp.bfloat16)
    origin = (core // 2) * 8

    lane = lax.broadcasted_iota(jnp.int32, (1, 256), 1)

    def limits(i):
        part = lane // HALF
        first = i * (2 * ROWS) + part * BLOCK
        time = first + core * HALF + lane % HALF
        reach = jnp.zeros((1, 256), jnp.int32)
        for n in range(4):
            figures = mine_ref[2 * i + n // 2, 3 * BLOCK :, :].astype(jnp.float32).astype(jnp.int32)
            at = 3 + 2 * (n % 2)
            mine = figures[:1, at : at + 1] * 16 + figures[:1, at + 1 : at + 2]
            reach = jnp.where(part == n, mine, reach)
        low = jnp.maximum(time - (WINDOW - 1), first - reach)
        low = jnp.maximum(low, 0)
        for bound in bounds:
            low = jnp.maximum(low, jnp.where(bound <= time, bound, 0))
        start = (2 * i + 2 - WIDTH) * ROWS
        return time - start, low - start

    def keys_of(i, widths):
        parts = []
        for w in widths:
            held = jnp.maximum(2 * i + 2 - WIDTH + w, 0)
            parts += [mine_ref[held, BLOCK : 2 * BLOCK, :], theirs_ref[held, BLOCK : 2 * BLOCK, :]]
        return jnp.concatenate(parts, axis=0)

    def scores_of(i, q, widths):
        return lax.dot_general(
            keys_of(i, widths), q, (((1,), (1,)), ((), ())), preferred_element_type=jnp.float32
        )

    def keep(s, w, time, low, s_ref, pos_ref, top):
        pos = pos_ref[w * 256 : (w + 1) * 256, :]
        pos = jnp.concatenate([pos, pos], axis=1)
        allowed = pos >= low
        if w >= WIDTH - 2:
            allowed = allowed & (pos <= time)
        s = jnp.where(allowed, s, MASKED)
        s_ref[pl.ds(pl.multiple_of(origin + w * 256, 8), 256), :] = s
        here = jnp.max(s.reshape(ROWS // 8, 8, 256), axis=0)
        return here if top is None else jnp.maximum(top, here)

    def queries_of(i):
        return jnp.concatenate([mine_ref[2 * i, :BLOCK, :], mine_ref[2 * i + 1, :BLOCK, :]], axis=0)

    def weigh(i, w, s_ref, m, acc):
        held = jnp.maximum(2 * i + 2 - WIDTH + w, 0)
        p = jnp.exp2(s_ref[w * 256 : (w + 1) * 256, :] * EXP_SCALE - m).astype(jnp.bfloat16)
        vt = jnp.concatenate(
            [mine_ref[held, 2 * BLOCK : 3 * BLOCK, :], theirs_ref[held, 2 * BLOCK : 3 * BLOCK, :]], axis=1
        )
        vt = jnp.concatenate([vt, ones], axis=0)
        o = lax.dot_general(vt, p, (((1,), (0,)), ((), ())), preferred_element_type=jnp.float32)
        return o if acc is None else acc + o

    def finish_top(top, m_ref):
        m_ref[...] = jnp.broadcast_to(jnp.max(top, axis=0, keepdims=True) * EXP_SCALE, (8, 256))

    def both(i, s_ref, m_ref, ahead, s_next, m_next, pos_next):
        time, low = limits(ahead)
        q = queries_of(ahead)
        m = m_ref[:1, :]
        top = acc = None
        s = scores_of(ahead, q, range(WIDTH))
        for w in range(WIDTH):
            acc = weigh(i, w, s_ref, m, acc)
            top = keep(s[w * 256 : (w + 1) * 256], w, time, low, s_next, pos_next, top)
        finish_top(top, m_next)
        o = (acc[:D_HEAD, :] / acc[D_HEAD : D_HEAD + 1, :]).T.astype(jnp.bfloat16)
        for part in range(4):
            out_ref[slot_ref[4 * i + part]] = o[part * HALF : (part + 1) * HALF]

    time, low = limits(0)
    q, top = queries_of(0), None
    for w in range(WIDTH - 2, WIDTH):
        top = keep(scores_of(0, q, (w,)), w, time, low, s0_ref, pos0_ref, top)
    finish_top(top, m0_ref)
    s0_ref[: (WIDTH - 2) * 256, :] = jnp.full(((WIDTH - 2) * 256, 256), MASKED, jnp.float32)

    def step(n, carry):
        both(2 * n, s0_ref, m0_ref, 2 * n + 1, s1_ref, m1_ref, pos1_ref)
        both(2 * n + 1, s1_ref, m1_ref, jnp.minimum(2 * n + 2, TILES - 1), s0_ref, m0_ref, pos0_ref)
        return carry

    lax.fori_loop(0, TILES // 2, step, 0)


def attention(mine, theirs, core, counts):
    smem = pl.BlockSpec(memory_space=pltpu.SMEM)
    vmem = pl.BlockSpec(memory_space=pltpu.VMEM)
    return pl.pallas_call(
        attend_kernel,
        in_specs=[smem, smem, vmem, vmem],
        out_specs=(vmem, smem),
        out_shape=(
            jax.ShapeDtypeStruct((N * SLOTS, HALF, D_HEAD), jnp.bfloat16),
            jax.ShapeDtypeStruct((4,), jnp.int32),
        ),
        scratch_shapes=[
            pltpu.VMEM((256 * WIDTH, 256), jnp.float32),
            pltpu.VMEM((256 * WIDTH, 256), jnp.float32),
            pltpu.VMEM((8, 256), jnp.float32),
            pltpu.VMEM((8, 256), jnp.float32),
            pltpu.VMEM((256 * WIDTH, 128), jnp.int32),
            pltpu.VMEM((256 * WIDTH, 128), jnp.int32),
            pltpu.SMEM((2 * N + 8,), jnp.int32),
        ],
        cost_estimate=pl.CostEstimate(
            flops=10 * 10**9, bytes_accessed=8 * 2**20, transcendentals=10**7
        ),
        compiler_params=pltpu.CompilerParams(vmem_limit_bytes=24 << 20),
        name="attend",
    )(core, counts, in_vmem(mine), in_vmem(theirs))


def in_hbm(array):
    return pltpu.with_memory_space_constraint(array, pltpu.HBM)


def in_vmem(array):
    return pltpu.with_memory_space_constraint(array, pltpu.VMEM)


def gather_kernel(in_ref, out_ref):
    slot = pl.program_id(0)
    rows = pl.ds(pl.multiple_of(slot * HALF, HALF), HALF)
    for h in range(HEADS):
        for c in range(2):
            out_ref[c * HALF : (c + 1) * HALF, h * D_HEAD : (h + 1) * D_HEAD] = in_ref[2 * h + c, rows, :]


def assemble(received):
    return pl.pallas_call(
        gather_kernel,
        grid=(SLOTS,),
        in_specs=[pl.BlockSpec(memory_space=pltpu.VMEM)],
        out_specs=pl.BlockSpec((BLOCK, HEADS * D_HEAD), lambda j: (j, 0)),
        out_shape=jax.ShapeDtypeStruct((SLOTS * BLOCK, HEADS * D_HEAD), jnp.bfloat16),
        compiler_params=pltpu.CompilerParams(vmem_limit_bytes=8 << 20),
        name="assemble",
    )(in_vmem(received))


def conv_kernel(figures_ref, bounds_ref, inner_ref, next_ref, tail_ref, weight_ref, bias_ref, out_ref, ext_ref):
    index, off, count = figures_ref[0], figures_ref[1], figures_ref[2]
    ext_ref[:8, :] = tail_ref[...].astype(jnp.float32)
    ext_ref[8 : 8 + ROWS, :] = inner_ref[...].astype(jnp.float32)
    ext_ref[8 + ROWS :, :] = next_ref[...].astype(jnp.float32)
    for block in range(SLOTS):
        slot = block - off

        @pl.when((slot >= 0) & (slot < count))
        def _(block=block, slot=slot):
            time = index * ROWS + block * BLOCK + lax.broadcasted_iota(jnp.int32, (BLOCK, 1), 0)
            start = jnp.zeros_like(time)
            for v in range(3):
                start = jnp.maximum(start, jnp.where(bounds_ref[v] <= time, bounds_ref[v], 0))
            since = time - start
            at = 8 + block * BLOCK
            total = bias_ref[...] + weight_ref[0:1, :] * ext_ref[at : at + BLOCK, :]
            for j in range(1, KERNEL):
                row = jnp.where(since >= j, ext_ref[at - j : at - j + BLOCK, :], 0.0)
                total = total + weight_ref[j : j + 1, :] * row
            out_ref[pl.ds(pl.multiple_of(slot * BLOCK, BLOCK), BLOCK), :] = (
                total / (1.0 + jnp.exp(-total))
            ).astype(jnp.bfloat16)

    for slot in range(1, SLOTS):

        @pl.when(slot >= count)
        def _(slot=slot):
            out_ref[slot * BLOCK : (slot + 1) * BLOCK, :] = jnp.zeros((BLOCK, out_ref.shape[1]), jnp.bfloat16)


def convolve(figures, bounds, inner, following, tail, weight, bias):
    channels = inner.shape[1]
    width = 512
    smem = pl.BlockSpec(memory_space=pltpu.SMEM)

    def wide(rows):
        return pl.BlockSpec((rows, width), lambda g: (0, g))

    return pl.pallas_call(
        conv_kernel,
        grid=(channels // width,),
        in_specs=[smem, smem, wide(ROWS), wide(BLOCK), wide(8), wide(KERNEL), wide(1)],
        out_specs=wide(SLOTS * BLOCK),
        out_shape=jax.ShapeDtypeStruct((SLOTS * BLOCK, channels), jnp.bfloat16),
        scratch_shapes=[pltpu.VMEM((8 + ROWS + BLOCK, width), jnp.float32)],
        cost_estimate=pl.CostEstimate(
            flops=10 * 10**9, bytes_accessed=6 * 2**20, transcendentals=2 * 10**6
        ),
        compiler_params=pltpu.CompilerParams(vmem_limit_bytes=24 << 20),
        name="conv",
    )(figures, bounds, inner, following, tail, weight, bias.reshape(1, -1))


def shards(queries, key_rows, values, inner_rows, conv_weight, conv_bias, segment_ids, block_reach, owner_counts):
    index = lax.axis_index("ctx").astype(jnp.int32)
    places = jnp.arange(N, dtype=jnp.int32)
    first = jnp.sum(jnp.where(places < index, owner_counts, 0))
    count = jnp.sum(jnp.where(places == index, owner_counts, 0))
    figures = jnp.stack([index, first - 2 * index, count, index])

    sent = pack(queries, key_rows, values, segment_ids, block_reach)
    mine = lax.all_to_all(sent, "ctx", 0, 0, tiled=True)
    theirs = lax.ppermute(mine, "ctx", [(i, i ^ 1) for i in range(N)])
    following = lax.ppermute(inner_rows[:BLOCK], "ctx", [(i, i - 1) for i in range(1, N)])
    tail = lax.ppermute(inner_rows[ROWS - 8 :], "ctx", [(i, i + 1) for i in range(N - 1)])
    theirs, tail = lax.optimization_barrier((theirs, tail))
    out, bounds = attention(mine, theirs, (index % 2).reshape(1), owner_counts)
    received = lax.all_to_all(out.reshape(N, SLOTS * HALF, D_HEAD), "ctx", 0, 0, tiled=True)
    attn_owned = assemble(received)
    conv_owned = convolve(figures, bounds, inner_rows, following, tail, conv_weight, conv_bias)
    return attn_owned, conv_owned


def solution(mesh):
    rows = P(("dp", "ctx"), None)
    flat = P(("dp", "ctx"))
    return jax.shard_map(
        shards,
        mesh=mesh,
        in_specs=(rows, rows, rows, rows, P(), P(), flat, flat, P("dp")),
        out_specs=(rows, rows),
        check_vma=False,
    )
```

time: 127 us -> 109 us (0.86)
  the two profiles are of different devices: /device:TPU:104 before, /device:TPU:224 now
where the time goes in v2:
time: 109 us; the launch traced here: 108 us
  blocking collectives  48.2 us (44%)
  Pallas kernels  31.3 us (29%)
  waiting for transfers between devices  12.3 us (11%)
  starting transfers between devices  9.75 us (9%)
  local copies, waits for them, and re-layouts  3.79 us (3%)
  between operations  1.36 us (1%)
  other arithmetic  1.32 us (1%)
    all_to_all x1, blocking collectives, shards(): mine = lax.all_to_all(sent, 'ctx', 0, 0, tiled=True)  48.2 us
    pallas_call x1, Pallas kernels, attention(): pl.pallas_call(attend_kernel, in_specs=[smem, smem, vmem, vmem], out_spec...  17.5 us
    all_to_all x1, waiting for transfers between devices, shards(): lax.all_to_all(out.reshape(N, SLOTS * HALF, D_HEAD), 'ctx', 0, 0, tiled=T...  11.2 us
    pallas_call x1, Pallas kernels, convolve(): pl.pallas_call(conv_kernel, grid=(channels // width,), in_specs=[smem, sm...  9.15 us
    all_to_all x1, starting transfers between devices, shards(): lax.all_to_all(out.reshape(N, SLOTS * HALF, D_HEAD), 'ctx', 0, 0, tiled=T...  6.06 us
    pallas_call x1, Pallas kernels, pack(): pl.pallas_call(pack_kernel, in_specs=[pl.BlockSpec(memory_space=pltpu.SME...  2.76 us
    unnamed x12, local copies, waits for them, and re-layouts  2.74 us
    ppermute x1, starting transfers between devices, shards(): lax.ppermute(inner_rows[ROWS - 8:], 'ctx', [(i, i + 1) for i in range(N -...  2.3 us
  transfers between devices with their start and end apart: 4, of which 3 were waited for; matrix products, arithmetic and copies ran while one was open for 2% of the time, Pallas kernels for 25%

profile of v2, /device:TPU:224, one launch (start us, length us, event | category | flops | bytes accessed | tf_op | source)
XLA Modules:
  0.0 108.1 jit_solution(3234881481859350732)
XLA Ops:
  0.6 2.8 %pack.1 = bf16[32,392,128]{2,1,0:T(8,128)(2,1)S(1)} custom-call(s32[2]{0:T(128)} %reach_ref.1, s32[2,128]{1,0:T(2,128)} %bitcast.9, bf16[256,2048]{1,0:T(8,128)(2,1)} %q_ref.1, bf16[256,2048]{1,0:T(8,128)(2,1)} %k_ref.1, bf16[256,2048]{1,0:T(8,128)(2,1)} %v_ref.1), custom_call_target="tpu_custom_call" | custom-call | tf_op jit(solution)/shard_map/pack/pallas_call | solution.py:76
  3.4 0.0 copy-start.1
  3.4 0.0 copy-start.3
  3.4 48.2 %all_to_all.10.mine_ref = bf16[32,392,128]{2,1,0:T(8,128)(2,1)S(1)} all-to-all(bf16[32,392,128]{2,1,0:T(8,128)(2,1)S(1)} %pack.1), channel_id=1, replica_groups=mesh['dp'=8,'ctx'=32] {'ctx'}, dimensions={0} | all-to-all | bytes 6422528 | tf_op jit(solution)/shard_map/all_to_all | solution.py:330
  51.6 0.1 collective-permute-start
  51.8 0.0 copy-done.1
  51.8 2.3 %collective-permute-start.1 = (bf16[8,4096]{1,0:T(8,128)(2,1)S(1)}, bf16[8,4096]{1,0:T(8,128)(2,1)S(1)}, u32[]{:S(2)}, u32[]{:S(2)}) collective-permute-start(bf16[8,4096]{1,0:T(8,128)(2,1)S(1)} %slice.6), channel_id=1, source_target_pairs={{0,1},{1,2},{2,3},{3,4},{4,5},{5,6},{6,7},{7,8},{8,9},{9,10},{10,1... | collective-permute-start | bytes 196616 | tf_op jit(solution)/shard_map/ppermute | solution.py:333
  54.1 1.0 slice.7
  55.1 1.3 %collective-permute-start.2 = (bf16[128,4096]{1,0:T(8,128)(2,1)}, bf16[128,4096]{1,0:T(8,128)(2,1)}, u32[]{:S(2)}, u32[]{:S(2)}) collective-permute-start(bf16[128,4096]{1,0:T(8,128)(2,1)} %slice.7), channel_id=1, source_target_pairs={{1,0},{2,1},{3,2},{4,3},{5,4},{6,5},{7,6},{8,7},{9,8},{10,9},{11,1... | collective-permute-start | bytes 3145736 | tf_op jit(solution)/shard_map/ppermute | solution.py:332
  56.4 0.8 collective-permute-done.1.tail_ref
  57.3 0.3 collective-permute-done.theirs_ref
  57.5 0.0 copy-done.3
  57.5 17.5 %attend.1 = (bf16[96,64,128]{2,1,0:T(8,128)(2,1)S(1)}, s32[4]{0:T(128)S(1)}) custom-call(s32[1]{0:T(128)} %bitcast.core_ref, s32[32]{0:T(128)S(1)} %copy-done.3, bf16[32,392,128]{2,1,0:T(8,128)(2,1)S(1)} %all_to_all.10.mine_ref, bf16[32,392,128]{2,1,0:T(8,128)(2,1)} %collective-permute-done.theirs_ref), custom_call_target="tpu_custom_call" | custom-call | flops 10000000000 | bytes 8388608 | tf_op jit(solution)/shard_map/attend/pallas_call | solution.py:215
  75.1 0.0 copy-start
  75.1 1.1 %copy-done = bf16[96,64,128]{2,1,0:T(8,128)(2,1)} copy-done((bf16[96,64,128]{2,1,0:T(8,128)(2,1)}, bf16[96,64,128]{2,1,0:T(8,128)(2,1)S(1)}, u32[]{:S(2)}) %copy-start) | copy-done | bytes 1572888
  76.2 0.0 copy-start.4
  76.2 0.0 copy-start.5
  76.2 6.1 %all-to-all-start.1 = ((bf16[32,192,128]{2,1,0:T(8,128)(2,1)}), bf16[32,192,128]{2,1,0:T(8,128)(2,1)S(1)}, u32[]{:S(2)}, u32[]{:S(2)}) async-start(bf16[32,192,128]{2,1,0:T(8,128)(2,1)} %bitcast.7), calls=%async_computation.1 | async-start | bytes 3145728 | tf_op jit(solution)/shard_map/all_to_all | solution.py:336
  82.3 0.7 fusion
  83.6 0.6 pad_add_fusion.figures_ref
  84.2 0.0 collective-permute-done.2.next_ref
  84.2 0.0 copy-done.4
  84.2 0.0 copy-done.5
  84.3 0.0 copy-start.2
  84.3 1.6 %copy-done.2 = bf16[256,4096]{1,0:T(8,128)(2,1)S(1)} copy-done((bf16[256,4096]{1,0:T(8,128)(2,1)S(1)}, bf16[256,4096]{1,0:T(8,128)(2,1)}, u32[]{:S(2)}) %copy-start.2) | copy-done | bytes 2097176
  85.8 9.1 %conv.1 = bf16[384,4096]{1,0:T(8,128)(2,1)} custom-call(s32[4]{0:T(128)S(1)} %pad_add_fusion.figures_ref, s32[4]{0:T(128)S(1)} %get-tuple-element.8.bounds_ref, bf16[256,4096]{1,0:T(8,128)(2,1)S(1)} %copy-done.2, bf16[128,4096]{1,0:T(8,128)(2,1)} %collective-permute-done.2.next_ref, bf16[8,4096]{1,0:T(8,128)(2,1)S(1)} %collective-permute-done.1.tail_ref, ...), custom_call_target="tpu_custom_call" | custom-call | flops 10000000000 | bytes 6291456 | tf_op jit(solution)/shard_map/conv/pallas_call | solution.py:307
  95.0 11.2 %all-to-all-done.1.in_ref = bf16[32,192,128]{2,1,0:T(8,128)(2,1)S(1)} async-done(((bf16[32,192,128]{2,1,0:T(8,128)(2,1)}), bf16[32,192,128]{2,1,0:T(8,128)(2,1)S(1)}, u32[]{:S(2)}, u32[]{:S(2)}) %all-to-all-start.1) | async-done | bytes 1572896 | tf_op jit(solution)/shard_map/all_to_all | solution.py:336
  106.2 1.9 %assemble.1 = bf16[384,2048]{1,0:T(8,128)(2,1)} custom-call(bf16[32,192,128]{2,1,0:T(8,128)(2,1)S(1)} %all-to-all-done.1.in_ref), custom_call_target="tpu_custom_call" | custom-call | tf_op jit(solution)/shard_map/assemble/pallas_call | solution.py:257
  (1 shorter events, 0.0 us)
Async XLA Ops:
  3.4 48.4 %copy-start.1 = (bf16[256,4096]{1,0:T(8,128)(2,1)S(1)}, bf16[256,4096]{1,0:T(8,128)(2,1)}, u32[]{:S(2)}) copy-start(bf16[256,4096]{1,0:T(8,128)(2,1)} %inner_ref.1) | copy-start | bytes 6291460
  3.4 54.1 %copy-start.3 = (s32[32]{0:T(128)S(1)}, s32[32]{0:T(128)}, u32[]{:S(2)}) copy-start(s32[32]{0:T(128)} %counts_ref.1) | copy-start | bytes 388
  51.6 5.9 %collective-permute-start = (bf16[32,392,128]{2,1,0:T(8,128)(2,1)S(1)}, bf16[32,392,128]{2,1,0:T(8,128)(2,1)}, u32[]{:S(2)}, u32[]{:S(2)}) collective-permute-start(bf16[32,392,128]{2,1,0:T(8,128)(2,1)S(1)} %all_to_all.10.mine_ref), channel_id=1, source_target_pairs={{0,1},{1,0},{2,3},{3,2},{4,5},{5,4},{6,7},{7,6},{8,9},{9,8},{10,11... | collective-permute-start | bytes 9633800 | tf_op jit(solution)/shard_map/ppermute | solution.py:331
  51.8 5.5 %collective-permute-start.1 = (bf16[8,4096]{1,0:T(8,128)(2,1)S(1)}, bf16[8,4096]{1,0:T(8,128)(2,1)S(1)}, u32[]{:S(2)}, u32[]{:S(2)}) collective-permute-start(bf16[8,4096]{1,0:T(8,128)(2,1)S(1)} %slice.6), channel_id=1, source_target_pairs={{0,1},{1,2},{2,3},{3,4},{4,5},{5,6},{6,7},{7,8},{8,9},{9,10},{10,1... | collective-permute-start | bytes 196616 | tf_op jit(solution)/shard_map/ppermute | solution.py:333
  55.1 29.1 %collective-permute-start.2 = (bf16[128,4096]{1,0:T(8,128)(2,1)}, bf16[128,4096]{1,0:T(8,128)(2,1)}, u32[]{:S(2)}, u32[]{:S(2)}) collective-permute-start(bf16[128,4096]{1,0:T(8,128)(2,1)} %slice.7), channel_id=1, source_target_pairs={{1,0},{2,1},{3,2},{4,3},{5,4},{6,5},{7,6},{8,7},{9,8},{10,9},{11,1... | collective-permute-start | bytes 3145736 | tf_op jit(solution)/shard_map/ppermute | solution.py:332
  75.1 1.1 %copy-start = (bf16[96,64,128]{2,1,0:T(8,128)(2,1)}, bf16[96,64,128]{2,1,0:T(8,128)(2,1)S(1)}, u32[]{:S(2)}) copy-start(bf16[96,64,128]{2,1,0:T(8,128)(2,1)S(1)} %get-tuple-element.7) | copy-start | bytes 4718596
  76.2 8.0 %copy-start.4 = (f32[4,4096]{1,0:T(4,128)S(1)}, f32[4,4096]{1,0:T(4,128)}, u32[]{:S(2)}) copy-start(f32[4,4096]{1,0:T(4,128)} %weight_ref.1) | copy-start | bytes 196612
  76.2 8.0 %copy-start.5 = (f32[4096]{0:T(1024)S(1)}, f32[4096]{0:T(1024)}, u32[]{:S(2)}) copy-start(f32[4096]{0:T(1024)} %param.14) | copy-start | bytes 49156
  76.2 30.0 %all-to-all-start.1 = ((bf16[32,192,128]{2,1,0:T(8,128)(2,1)}), bf16[32,192,128]{2,1,0:T(8,128)(2,1)S(1)}, u32[]{:S(2)}, u32[]{:S(2)}) async-start(bf16[32,192,128]{2,1,0:T(8,128)(2,1)} %bitcast.7), calls=%async_computation.1 | async-start | bytes 3145728 | tf_op jit(solution)/shard_map/all_to_all | solution.py:336
  84.3 1.6 %copy-start.2 = (bf16[256,4096]{1,0:T(8,128)(2,1)S(1)}, bf16[256,4096]{1,0:T(8,128)(2,1)}, u32[]{:S(2)}) copy-start(bf16[256,4096]{1,0:T(8,128)(2,1)} %inner_ref.1) | copy-start | bytes 6291460

commit v3 on v2

--- a/solution.py
+++ b/solution.py
@@ -20,12 +20,14 @@
 MSG = 3 * BLOCK + 8
 TILES = N // 2
 WIDTH = 10
+WIDTHS = (6, 8, 10)
+PIECES = 4
 EXP_SCALE = math.log2(math.e) / math.sqrt(D_HEAD)
 MASKED = -1e30
 GROUP = 4
 
 
-def pack_kernel(reach_ref, seg_ref, q_ref, k_ref, v_ref, out_ref, held_ref, sems):
+def pack_kernel(reach_ref, seg_ref, q_ref, k_ref, v_ref, inner_ref, out_ref, lead_ref, last_ref, held_ref, sems, row_sems):
     width = GROUP * D_HEAD
     copies = {}
     for g in range(HEADS // GROUP):
@@ -35,6 +37,10 @@
                 ref.at[:, columns], held_ref.at[n, :, columns], sems.at[g, n]
             )
             copies[g, n].start()
+    lead = pltpu.make_async_copy(inner_ref.at[pl.ds(0, BLOCK)], lead_ref, row_sems.at[0])
+    last = pltpu.make_async_copy(inner_ref.at[pl.ds(ROWS - 8, 8)], last_ref, row_sems.at[1])
+    lead.start()
+    last.start()
     seg = seg_ref[...]
     lane = lax.broadcasted_iota(jnp.int32, (8, 128), 1)
     meta = jnp.zeros((8, 128), jnp.int32)
@@ -68,30 +74,46 @@
                         ]
     for e in range(N):
         out_ref[e, 3 * BLOCK :, :] = meta
-
-
-def pack(q, k, v, seg, reach):
+    lead.wait()
+    last.wait()
+
+
+def pack(q, k, v, seg, reach, inner):
     anywhere = pl.BlockSpec(memory_space=pl.ANY)
     vmem = pl.BlockSpec(memory_space=pltpu.VMEM)
     return pl.pallas_call(
         pack_kernel,
-        in_specs=[pl.BlockSpec(memory_space=pltpu.SMEM), vmem, anywhere, anywhere, anywhere],
-        out_specs=vmem,
-        out_shape=pltpu.VMEM((N, MSG, D_HEAD), jnp.bfloat16),
+        in_specs=[pl.BlockSpec(memory_space=pltpu.SMEM), vmem, anywhere, anywhere, anywhere, anywhere],
+        out_specs=(vmem, vmem, vmem),
+        out_shape=(
+            pltpu.VMEM((N, MSG, D_HEAD), jnp.bfloat16),
+            pltpu.VMEM((BLOCK, inner.shape[1]), jnp.bfloat16),
+            pltpu.VMEM((8, inner.shape[1]), jnp.bfloat16),
+        ),
         scratch_shapes=[
             pltpu.VMEM((3, ROWS, HEADS * D_HEAD), jnp.bfloat16),
             pltpu.SemaphoreType.DMA((HEADS // GROUP, 3)),
+            pltpu.SemaphoreType.DMA((2,)),
         ],
         compiler_params=pltpu.CompilerParams(vmem_limit_bytes=8 << 20),
         name="pack",
-    )(in_hbm(reach), in_hbm(seg.reshape(2, 128)), in_hbm(q), in_hbm(k), in_hbm(v))
+    )(in_hbm(reach), in_hbm(seg.reshape(2, 128)), in_hbm(q), in_hbm(k), in_hbm(v), in_hbm(inner))
 
 
 def attend_kernel(
-    core_ref, counts_ref, mine_ref, theirs_ref, out_ref, bounds_ref,
+    core_ref, counts_ref, mine_ref, other_ref, out_ref, bounds_ref, theirs_ref, sems, need_ref,
     s0_ref, s1_ref, m0_ref, m1_ref, pos0_ref, pos1_ref, slot_ref,
 ):
     core = core_ref[0]
+    size = N // PIECES
+    pieces = [
+        pltpu.make_async_copy(
+            other_ref.at[pl.ds(p * size, size)], theirs_ref.at[pl.ds(p * size, size)], sems.at[p]
+        )
+        for p in range(PIECES)
+    ]
+    for piece in pieces:
+        piece.start()
 
     def fill(e, first):
         count = counts_ref[e]
@@ -113,6 +135,22 @@
     lane1 = lax.broadcasted_iota(jnp.int32, (1, 128), 1)
     for v in range(3):
         bounds_ref[v] = jnp.sum(jnp.where(lane1 == v, totals, 0))
+
+    def lowest(first, reach):
+        low = jnp.maximum(jnp.maximum(first - (WINDOW - 1), first - reach), 0)
+        for bound in bounds:
+            low = jnp.maximum(low, jnp.where(bound <= first, bound, 0))
+        return low
+
+    source = lax.broadcasted_iota(jnp.int32, (N, 1), 0)
+    least = [
+        lowest(source * ROWS + b * BLOCK, meta[:, 3 + 2 * b : 4 + 2 * b] * 16 + meta[:, 4 + 2 * b : 5 + 2 * b])
+        for b in range(2)
+    ]
+    least = jnp.minimum(least[0], least[1])
+    for i in range(TILES):
+        need_ref[i] = 2 * i + 2 - jnp.min(jnp.where(source // 2 == i, least, N * ROWS)) // ROWS
+    need_ref[TILES] = 0
 
     for ref in (pos0_ref, pos1_ref):
         key = lax.broadcasted_iota(jnp.int32, (2 * BLOCK, 128), 0)
@@ -180,33 +218,62 @@
     def finish_top(top, m_ref):
         m_ref[...] = jnp.broadcast_to(jnp.max(top, axis=0, keepdims=True) * EXP_SCALE, (8, 256))
 
-    def both(i, s_ref, m_ref, ahead, s_next, m_next, pos_next):
+    def both(i, s_ref, m_ref, ahead, s_next, m_next, pos_next, width):
         time, low = limits(ahead)
         q = queries_of(ahead)
         m = m_ref[:1, :]
         top = acc = None
-        s = scores_of(ahead, q, range(WIDTH))
-        for w in range(WIDTH):
+        skip = WIDTH - width
+        s = scores_of(ahead, q, range(skip, WIDTH))
+        for w in range(skip, WIDTH):
             acc = weigh(i, w, s_ref, m, acc)
-            top = keep(s[w * 256 : (w + 1) * 256], w, time, low, s_next, pos_next, top)
+            top = keep(s[(w - skip) * 256 : (w - skip + 1) * 256], w, time, low, s_next, pos_next, top)
         finish_top(top, m_next)
         o = (acc[:D_HEAD, :] / acc[D_HEAD : D_HEAD + 1, :]).T.astype(jnp.bfloat16)
         for part in range(4):
             out_ref[slot_ref[4 * i + part]] = o[part * HALF : (part + 1) * HALF]
 
+    pieces[0].wait()
     time, low = limits(0)
     q, top = queries_of(0), None
     for w in range(WIDTH - 2, WIDTH):
         top = keep(scores_of(0, q, (w,)), w, time, low, s0_ref, pos0_ref, top)
     finish_top(top, m0_ref)
-    s0_ref[: (WIDTH - 2) * 256, :] = jnp.full(((WIDTH - 2) * 256, 256), MASKED, jnp.float32)
-
-    def step(n, carry):
-        both(2 * n, s0_ref, m0_ref, 2 * n + 1, s1_ref, m1_ref, pos1_ref)
-        both(2 * n + 1, s1_ref, m1_ref, jnp.minimum(2 * n + 2, TILES - 1), s0_ref, m0_ref, pos0_ref)
+
+    def blank(w, carry):
+        s0_ref[pl.ds(pl.multiple_of(w * 256, 256), 256), :] = jnp.full((256, 256), MASKED, jnp.float32)
         return carry
 
-    lax.fori_loop(0, TILES // 2, step, 0)
+    lax.fori_loop(0, WIDTH - 2, blank, 0)
+
+    def most(n):
+        return jnp.maximum(jnp.maximum(need_ref[2 * n], need_ref[2 * n + 1]), need_ref[2 * n + 2])
+
+    def step(n, need):
+        for p in range(1, PIECES):
+            @pl.when(n == (p * size - 5 + 3) // 4)
+            def _(p=p):
+                pieces[p].wait()
+
+        below = 0
+        for width in WIDTHS:
+
+            @pl.when((need > below) & (need <= width))
+            def _(width=width):
+                both(2 * n, s0_ref, m0_ref, 2 * n + 1, s1_ref, m1_ref, pos1_ref, width)
+                both(2 * n + 1, s1_ref, m1_ref, jnp.minimum(2 * n + 2, TILES - 1), s0_ref, m0_ref, pos0_ref, width)
+
+            below = width
+        later = most(jnp.minimum(n + 1, TILES // 2 - 1))
+        for narrow, wide in zip(WIDTHS[:-1], WIDTHS[1:]):
+
+            @pl.when((need <= narrow) & (later > narrow))
+            def _(narrow=narrow, wide=wide):
+                lax.fori_loop(WIDTH - wide, WIDTH - narrow, blank, 0)
+
+        return later
+
+    lax.fori_loop(0, TILES // 2, step, most(0))
 
 
 def attention(mine, theirs, core, counts):
@@ -214,13 +281,16 @@
     vmem = pl.BlockSpec(memory_space=pltpu.VMEM)
     return pl.pallas_call(
         attend_kernel,
-        in_specs=[smem, smem, vmem, vmem],
+        in_specs=[smem, smem, vmem, pl.BlockSpec(memory_space=pl.ANY)],
         out_specs=(vmem, smem),
         out_shape=(
-            jax.ShapeDtypeStruct((N * SLOTS, HALF, D_HEAD), jnp.bfloat16),
+            pltpu.HBM((N * SLOTS, HALF, D_HEAD), jnp.bfloat16),
             jax.ShapeDtypeStruct((4,), jnp.int32),
         ),
         scratch_shapes=[
+            pltpu.VMEM((N, MSG, D_HEAD), jnp.bfloat16),
+            pltpu.SemaphoreType.DMA((PIECES,)),
+            pltpu.SMEM((TILES + 1,), jnp.int32),
             pltpu.VMEM((256 * WIDTH, 256), jnp.float32),
             pltpu.VMEM((256 * WIDTH, 256), jnp.float32),
             pltpu.VMEM((8, 256), jnp.float32),
@@ -234,7 +304,7 @@
         ),
         compiler_params=pltpu.CompilerParams(vmem_limit_bytes=24 << 20),
         name="attend",
-    )(core, counts, in_vmem(mine), in_vmem(theirs))
+    )(core, counts, in_vmem(mine), in_hbm(theirs))
 
 
 def in_hbm(array):
@@ -326,11 +396,12 @@
     count = jnp.sum(jnp.where(places == index, owner_counts, 0))
     figures = jnp.stack([index, first - 2 * index, count, index])
 
-    sent = pack(queries, key_rows, values, segment_ids, block_reach)
+    sent, lead, last = pack(queries, key_rows, values, segment_ids, block_reach, inner_rows)
     mine = lax.all_to_all(sent, "ctx", 0, 0, tiled=True)
+    mine, lead, last = lax.optimization_barrier((mine, lead, last))
     theirs = lax.ppermute(mine, "ctx", [(i, i ^ 1) for i in range(N)])
-    following = lax.ppermute(inner_rows[:BLOCK], "ctx", [(i, i - 1) for i in range(1, N)])
-    tail = lax.ppermute(inner_rows[ROWS - 8 :], "ctx", [(i, i + 1) for i in range(N - 1)])
+    following = lax.ppermute(lead, "ctx", [(i, i - 1) for i in range(1, N)])
+    tail = lax.ppermute(last, "ctx", [(i, i + 1) for i in range(N - 1)])
     theirs, tail = lax.optimization_barrier((theirs, tail))
     out, bounds = attention(mine, theirs, (index % 2).reshape(1), owner_counts)
     received = lax.all_to_all(out.reshape(N, SLOTS * HALF, D_HEAD), "ctx", 0, 0, tiled=True)

time: 109 us -> 106 us (0.972)
  the two profiles are of different devices: /device:TPU:224 before, /device:TPU:96 now
where the time goes in v3:
time: 106 us; the launch traced here: 105 us
  blocking collectives  48.2 us (45%)
  Pallas kernels  30.4 us (29%)
  waiting for transfers between devices  13.4 us (13%)
  starting transfers between devices  8.7 us (8%)
  local copies, waits for them, and re-layouts  1.61 us (2%)
  between operations  1.36 us (1%)
  other arithmetic  1.32 us (1%)
    all_to_all x1, blocking collectives, shards(): mine = lax.all_to_all(sent, 'ctx', 0, 0, tiled=True)  48.2 us
    pallas_call x1, Pallas kernels, attention(): pl.pallas_call(attend_kernel, in_specs=[smem, smem, vmem, pl.BlockSpec(me...  16.3 us
    all_to_all x1, waiting for transfers between devices, shards(): lax.all_to_all(out.reshape(N, SLOTS * HALF, D_HEAD), 'ctx', 0, 0, tiled=T...  11.2 us
    pallas_call x1, Pallas kernels, convolve(): pl.pallas_call(conv_kernel, grid=(channels // width,), in_specs=[smem, sm...  9.15 us
    all_to_all x1, starting transfers between devices, shards(): lax.all_to_all(out.reshape(N, SLOTS * HALF, D_HEAD), 'ctx', 0, 0, tiled=T...  5 us
    pallas_call x1, Pallas kernels, pack(): pl.pallas_call(pack_kernel, in_specs=[pl.BlockSpec(memory_space=pltpu.SME...  3.1 us
    ppermute x1, starting transfers between devices, shards(): tail = lax.ppermute(last, 'ctx', [(i, i + 1) for i in range(N - 1)])  2.29 us
  transfers between devices with their start and end apart: 4, of which 3 were waited for; matrix products, arithmetic and copies ran while one was open for 1% of the time, Pallas kernels for 24%

profile of v3, /device:TPU:96, one launch (start us, length us, event | category | flops | bytes accessed | tf_op | source)
XLA Modules:
  0.0 105.0 jit_solution(3537455197071315413)
XLA Ops:
  0.6 3.1 %pack.1 = (bf16[32,392,128]{2,1,0:T(8,128)(2,1)S(1)}, bf16[128,4096]{1,0:T(8,128)(2,1)S(1)}, bf16[8,4096]{1,0:T(8,128)(2,1)S(1)}) custom-call(s32[2]{0:T(128)} %reach_ref.1, s32[2,128]{1,0:T(2,128)} %bitcast.9, bf16[256,2048]{1,0:T(8,128)(2,1)} %q_ref.1, bf16[256,2048]{1,0:T(8,128)(2,1)} %k_ref.1, bf16[256,2048]{1,0:T(8,128)(2,1)} %v_ref.1, ...), custom_call_target="tpu_custom_call" | custom-call | tf_op jit(solution)/shard_map/pack/pallas_call | solution.py:84
  3.7 0.0 copy-start.2
  3.7 0.0 copy-start.1
  3.8 48.2 %all_to_all.10.mine_ref = bf16[32,392,128]{2,1,0:T(8,128)(2,1)S(1)} all-to-all(bf16[32,392,128]{2,1,0:T(8,128)(2,1)S(1)} %get-tuple-element.12), channel_id=1, replica_groups=mesh['dp'=8,'ctx'=32] {'ctx'}, dimensions={0} | all-to-all | bytes 6422528 | tf_op jit(solution)/shard_map/all_to_all | solution.py:400
  52.0 0.0 copy-done.2
  52.0 0.1 collective-permute-start
  52.1 2.3 %collective-permute-start.1 = (bf16[8,4096]{1,0:T(8,128)(2,1)S(1)}, bf16[8,4096]{1,0:T(8,128)(2,1)S(1)}, u32[]{:S(2)}, u32[]{:S(2)}) collective-permute-start(bf16[8,4096]{1,0:T(8,128)(2,1)S(1)} %get-tuple-element.16), channel_id=1, source_target_pairs={{0,1},{1,2},{2,3},{3,4},{4,5},{5,6},{6,7},{7,8},{8,9},{9,10},{10,1... | collective-permute-start | bytes 196616 | tf_op jit(solution)/shard_map/ppermute | solution.py:404
  54.4 1.3 %collective-permute-start.2 = (bf16[128,4096]{1,0:T(8,128)(2,1)}, bf16[128,4096]{1,0:T(8,128)(2,1)}, u32[]{:S(2)}, u32[]{:S(2)}) collective-permute-start(bf16[128,4096]{1,0:T(8,128)(2,1)} %copy-done.2), channel_id=1, source_target_pairs={{1,0},{2,1},{3,2},{4,3},{5,4},{6,5},{7,6},{8,7},{9,8},{10,9},{11,1... | collective-permute-start | bytes 3145736 | tf_op jit(solution)/shard_map/ppermute | solution.py:403
  55.7 1.9 %collective-permute-done.1.tail_ref = bf16[8,4096]{1,0:T(8,128)(2,1)S(1)} collective-permute-done((bf16[8,4096]{1,0:T(8,128)(2,1)S(1)}, bf16[8,4096]{1,0:T(8,128)(2,1)S(1)}, u32[]{:S(2)}, u32[]{:S(2)}) %collective-permute-start.1) | collective-permute-done | bytes 65568 | tf_op jit(solution)/shard_map/ppermute | solution.py:404
  57.6 0.3 collective-permute-done.other_ref
  57.9 0.0 copy-done.1
  57.9 16.3 %attend.1 = (bf16[96,64,128]{2,1,0:T(8,128)(2,1)}, s32[4]{0:T(128)S(1)}) custom-call(s32[1]{0:T(128)} %bitcast.core_ref, s32[32]{0:T(128)S(1)} %copy-done.1, bf16[32,392,128]{2,1,0:T(8,128)(2,1)S(1)} %all_to_all.10.mine_ref, bf16[32,392,128]{2,1,0:T(8,128)(2,1)} %collective-permute-done.other_ref), custom_call_target="tpu_custom_call" | custom-call | flops 10000000000 | bytes 8388608 | tf_op jit(solution)/shard_map/attend/pallas_call | solution.py:282
  74.2 0.0 copy-start.3
  74.2 0.0 copy-start.4
  74.2 5.0 %all-to-all-start.1 = ((bf16[32,192,128]{2,1,0:T(8,128)(2,1)}), bf16[32,192,128]{2,1,0:T(8,128)(2,1)S(1)}, u32[]{:S(2)}, u32[]{:S(2)}) async-start(bf16[32,192,128]{2,1,0:T(8,128)(2,1)} %bitcast.8), calls=%async_computation.1 | async-start | bytes 3145728 | tf_op jit(solution)/shard_map/all_to_all | solution.py:407
  79.2 0.7 fusion
  80.6 0.6 pad_add_fusion.figures_ref
  81.2 0.0 collective-permute-done.2.next_ref
  81.2 0.0 copy-done.3
  81.2 0.0 copy-done.4
  81.2 0.0 copy-start
  81.2 1.6 %copy-done = bf16[256,4096]{1,0:T(8,128)(2,1)S(1)} copy-done((bf16[256,4096]{1,0:T(8,128)(2,1)S(1)}, bf16[256,4096]{1,0:T(8,128)(2,1)}, u32[]{:S(2)}) %copy-start) | copy-done | bytes 2097176
  82.8 9.2 %conv.1 = bf16[384,4096]{1,0:T(8,128)(2,1)} custom-call(s32[4]{0:T(128)S(1)} %pad_add_fusion.figures_ref, s32[4]{0:T(128)S(1)} %get-tuple-element.19.bounds_ref, bf16[256,4096]{1,0:T(8,128)(2,1)S(1)} %copy-done, bf16[128,4096]{1,0:T(8,128)(2,1)} %collective-permute-done.2.next_ref, bf16[8,4096]{1,0:T(8,128)(2,1)S(1)} %collective-permute-done.1.tail_ref, ...), custom_call_target="tpu_custom_call" | custom-call | flops 10000000000 | bytes 6291456 | tf_op jit(solution)/shard_map/conv/pallas_call | solution.py:377
  92.0 11.2 %all-to-all-done.1.in_ref = bf16[32,192,128]{2,1,0:T(8,128)(2,1)S(1)} async-done(((bf16[32,192,128]{2,1,0:T(8,128)(2,1)}), bf16[32,192,128]{2,1,0:T(8,128)(2,1)S(1)}, u32[]{:S(2)}, u32[]{:S(2)}) %all-to-all-start.1) | async-done | bytes 1572896 | tf_op jit(solution)/shard_map/all_to_all | solution.py:407
  103.2 1.9 %assemble.1 = bf16[384,2048]{1,0:T(8,128)(2,1)} custom-call(bf16[32,192,128]{2,1,0:T(8,128)(2,1)S(1)} %all-to-all-done.1.in_ref), custom_call_target="tpu_custom_call" | custom-call | tf_op jit(solution)/shard_map/assemble/pallas_call | solution.py:327
Async XLA Ops:
  3.7 48.2 %copy-start.2 = (bf16[128,4096]{1,0:T(8,128)(2,1)}, bf16[128,4096]{1,0:T(8,128)(2,1)S(1)}, u32[]{:S(2)}) copy-start(bf16[128,4096]{1,0:T(8,128)(2,1)S(1)} %get-tuple-element.20) | copy-start | bytes 3145732
  3.7 54.1 %copy-start.1 = (s32[32]{0:T(128)S(1)}, s32[32]{0:T(128)}, u32[]{:S(2)}) copy-start(s32[32]{0:T(128)} %counts_ref.1) | copy-start | bytes 388
  52.0 5.9 %collective-permute-start = (bf16[32,392,128]{2,1,0:T(8,128)(2,1)S(1)}, bf16[32,392,128]{2,1,0:T(8,128)(2,1)}, u32[]{:S(2)}, u32[]{:S(2)}) collective-permute-start(bf16[32,392,128]{2,1,0:T(8,128)(2,1)S(1)} %all_to_all.10.mine_ref), channel_id=1, source_target_pairs={{0,1},{1,0},{2,3},{3,2},{4,5},{5,4},{6,7},{7,6},{8,9},{9,8},{10,11... | collective-permute-start | bytes 9633800 | tf_op jit(solution)/shard_map/ppermute | solution.py:402
  52.1 5.5 %collective-permute-start.1 = (bf16[8,4096]{1,0:T(8,128)(2,1)S(1)}, bf16[8,4096]{1,0:T(8,128)(2,1)S(1)}, u32[]{:S(2)}, u32[]{:S(2)}) collective-permute-start(bf16[8,4096]{1,0:T(8,128)(2,1)S(1)} %get-tuple-element.16), channel_id=1, source_target_pairs={{0,1},{1,2},{2,3},{3,4},{4,5},{5,6},{6,7},{7,8},{8,9},{9,10},{10,1... | collective-permute-start | bytes 196616 | tf_op jit(solution)/shard_map/ppermute | solution.py:404
  54.4 26.8 %collective-permute-start.2 = (bf16[128,4096]{1,0:T(8,128)(2,1)}, bf16[128,4096]{1,0:T(8,128)(2,1)}, u32[]{:S(2)}, u32[]{:S(2)}) collective-permute-start(bf16[128,4096]{1,0:T(8,128)(2,1)} %copy-done.2), channel_id=1, source_target_pairs={{1,0},{2,1},{3,2},{4,3},{5,4},{6,5},{7,6},{8,7},{9,8},{10,9},{11,1... | collective-permute-start | bytes 3145736 | tf_op jit(solution)/shard_map/ppermute | solution.py:403
  74.2 7.0 %copy-start.3 = (f32[4,4096]{1,0:T(4,128)S(1)}, f32[4,4096]{1,0:T(4,128)}, u32[]{:S(2)}) copy-start(f32[4,4096]{1,0:T(4,128)} %weight_ref.1) | copy-start | bytes 196612
  74.2 7.0 %copy-start.4 = (f32[4096]{0:T(1024)S(1)}, f32[4096]{0:T(1024)}, u32[]{:S(2)}) copy-start(f32[4096]{0:T(1024)} %param.14) | copy-start | bytes 49156
  74.2 28.9 %all-to-all-start.1 = ((bf16[32,192,128]{2,1,0:T(8,128)(2,1)}), bf16[32,192,128]{2,1,0:T(8,128)(2,1)S(1)}, u32[]{:S(2)}, u32[]{:S(2)}) async-start(bf16[32,192,128]{2,1,0:T(8,128)(2,1)} %bitcast.8), calls=%async_computation.1 | async-start | bytes 3145728 | tf_op jit(solution)/shard_map/all_to_all | solution.py:407
  81.2 1.6 %copy-start = (bf16[256,4096]{1,0:T(8,128)(2,1)S(1)}, bf16[256,4096]{1,0:T(8,128)(2,1)}, u32[]{:S(2)}) copy-start(bf16[256,4096]{1,0:T(8,128)(2,1)} %inner_ref.3) | copy-start | bytes 6291460
